TPU v7x, 256 devices: a whole 4x4x8 slice. The times are simulated.
256 devices in a mesh: row: 16 (over y, z_hi), col: 16 (over x, z_lo, core).
Axes of the slice: x: 4, y: 4, z: 8 (z_hi: 4, z_lo: 2; z = z_hi * 2 + z_lo), core: 2. Of those that a mesh axis runs over, the one named last changes fastest.
Arguments:
- left_act: bfloat16 [1536, 128], P(('row', 'col')), may hold values from -540 to 540
- right_act: bfloat16 [1536, 128], P(('row', 'col')), may hold values from -6 to 6
- norm_gain: float32 [128], replicated, may hold values from 0.25 to 1.75
- norm_bias: float32 [128], replicated, may hold values from -3 to 3
- w_in: bfloat16 [128, 512], replicated, may hold values from -0.5 to 0.5
- b_in: float32 [512], replicated, may hold values from -3 to 3
- w_out: bfloat16 [512, 128], replicated, may hold values from -0.25 to 0.25
- w_bins: bfloat16 [128, 64], replicated, may hold values from -0.5 to 0.5
- labels: int32 [1536, 1536], P('row', 'col'), may hold values from 0 to 63, as said below
Outputs:
- grad_left: float32 [1536, 128], P(('row', 'col'))
- grad_right: float32 [1536, 128], P('col')
- grad_w_in: float32 [128, 512], replicated
- grad_w_out: float32 [512, 128], replicated
- grad_w_bins: float32 [128, 64], replicated
Inputs may be any that keep to these rules, and one draw needn't show every extreme that they name: labels is symmetric: labels[i, j] equals labels[j, i].
All inputs are finite; a program needn't handle non-finite values.
Results may differ from a plain program's by a relative error of at most 0.00039.
Values may be sent and summed in bfloat16 or wider, within the bound.
No kernel may reach another device: no remote copies, remote signals or barrier semaphores. Data moves between devices by JAX's collectives and lax.ppermute only.
A program may use at most 64 MiB of HBM per device.

v0:
```python
import jax
import jax.numpy as jnp
from jax import lax
from jax.sharding import PartitionSpec as P


def from_everyone(value, axis):
    count = lax.axis_size(axis)
    return lax.all_to_all(
        jnp.broadcast_to(value[None], (count, *value.shape)), axis, 0, 0, tiled=True
    )


def laid_out(pieces, dim):
    shape = list(pieces.shape[1:])
    shape[dim] *= pieces.shape[0]
    return jnp.moveaxis(pieces, 0, dim).reshape(shape)


def gather_directly(value, axis, dim):
    pieces = from_everyone(value, axis)
    return laid_out(pieces, dim)


def picked(value, axis, root):
    return lax.dynamic_index_in_dim(lax.all_gather(value, axis), root, 0, keepdims=False)


def over_copies(value, axis):
    return from_everyone(value, axis).sum(axis=0)


def inner(first, second):
    return lax.dot_general(
        first, second, (((0,), (0,)), ((), ())), preferred_element_type=jnp.float32
    )


def outer(first, second):
    return lax.dot_general(
        first, second, (((1,), (1,)), ((), ())), preferred_element_type=jnp.float32
    )


def transition(left_rows, right_cols, gain, bias, w_in, b_in, w_out):
    summed = (
        left_rows.astype(jnp.float32)[:, None, :] + right_cols.astype(jnp.float32)[None, :, :]
    ).reshape(-1, left_rows.shape[1])
    center = summed - jnp.mean(summed, axis=-1, keepdims=True)
    inv_scale = lax.rsqrt(jnp.mean(center * center, axis=-1, keepdims=True) + 1e-05)
    normal_form = center * inv_scale
    normed = (normal_form * gain + bias).astype(jnp.bfloat16)
    pre_act = jnp.dot(normed, w_in, preferred_element_type=jnp.float32) + b_in
    hidden = (pre_act * jax.nn.sigmoid(pre_act)).astype(jnp.bfloat16)
    updated = (summed + jnp.dot(hidden, w_out, preferred_element_type=jnp.float32)).astype(
        jnp.bfloat16
    )
    return (normal_form, inv_scale, normed, pre_act, hidden, updated)


def pair_backward(sym, bin_labels, parts, gain, w_in, w_out, w_bins):
    normal_form, inv_scale, normed, pre_act, hidden, updated = parts
    shifted = sym - jnp.max(sym, axis=-1, keepdims=True)
    expo = jnp.exp(shifted)
    probs = expo / jnp.sum(expo, axis=-1, keepdims=True)
    onehot = (bin_labels[..., None] == lax.iota(jnp.int32, sym.shape[-1])).astype(jnp.float32)
    logit_grad = (2.0 * (probs - onehot)).reshape(-1, sym.shape[-1]).astype(jnp.bfloat16)
    grad_bins = inner(updated, logit_grad)
    upd_grad = outer(logit_grad, w_bins)
    upd_half = upd_grad.astype(jnp.bfloat16)
    grad_out = inner(hidden, upd_half)
    hid_grad = outer(upd_half, w_out)
    sigma = jax.nn.sigmoid(pre_act)
    pre_grad = (hid_grad * sigma * (1.0 + pre_act * (1.0 - sigma))).astype(jnp.bfloat16)
    grad_in = inner(normed, pre_grad)
    norm_grad = outer(pre_grad, w_in) * gain
    pair_grad = (
        inv_scale
        * (
            norm_grad
            - jnp.mean(norm_grad, axis=-1, keepdims=True)
            - normal_form * jnp.mean(norm_grad * normal_form, axis=-1, keepdims=True)
        )
        + upd_grad
    )
    return (grad_in, grad_out, grad_bins, pair_grad)


def on_device(left_act, right_act, norm_gain, norm_bias, w_in, b_in, w_out, w_bins, labels):
    tile_rows, tile_cols = labels.shape
    width = left_act.shape[1]
    stacked = jnp.stack([left_act, right_act])
    row_block = gather_directly(stacked, "col", 1)
    fanout = lax.axis_size("row") // lax.axis_size("col")
    pieces = picked(row_block, "row", lax.axis_index("col") * fanout + 0)
    stride_rows = 8
    groups = tile_rows // stride_rows

    def advance(running, record):
        left_rows, right_rows, bin_labels = record
        own_parts = transition(left_rows, pieces[1], norm_gain, norm_bias, w_in, b_in, w_out)
        own_logits = jnp.dot(own_parts[5], w_bins, preferred_element_type=jnp.float32).reshape(
            stride_rows, tile_cols, -1
        )
        far_parts = transition(pieces[0], right_rows, norm_gain, norm_bias, w_in, b_in, w_out)
        far_logits = jnp.dot(far_parts[5], w_bins, preferred_element_type=jnp.float32).reshape(
            tile_cols, stride_rows, -1
        )
        sym = own_logits + jnp.transpose(far_logits, (1, 0, 2))
        grads = pair_backward(sym, bin_labels, own_parts, norm_gain, w_in, w_out, w_bins)
        pair_grad = grads[3].reshape(stride_rows, tile_cols, width)
        running = (
            running[0] + grads[0],
            running[1] + grads[1],
            running[2] + grads[2],
            running[3] + jnp.sum(pair_grad, axis=0),
        )
        return (running, jnp.sum(pair_grad, axis=1))

    start = (
        jnp.zeros((width, w_in.shape[1]), jnp.float32),
        jnp.zeros((w_in.shape[1], width), jnp.float32),
        jnp.zeros((width, w_bins.shape[1]), jnp.float32),
        jnp.zeros((tile_cols, width), jnp.float32),
    )
    records = (
        row_block[0].reshape(groups, stride_rows, width),
        row_block[1].reshape(groups, stride_rows, width),
        labels.reshape(groups, stride_rows, tile_cols),
    )
    running, left_terms = lax.scan(advance, start, records)
    grad_left = lax.psum_scatter(
        left_terms.reshape(tile_rows, width), "col", scatter_dimension=0, tiled=True
    )
    grad_right = over_copies(running[3], "row")
    grad_in, grad_out, grad_bins = lax.psum((running[0], running[1], running[2]), ("row", "col"))
    residues = tile_rows * lax.axis_size("row")
    return (grad_left, grad_right, grad_in / residues, grad_out / residues, grad_bins / residues)


def solution(mesh):
    placed = (
        P(("row", "col"), None),
        P(("row", "col"), None),
        P(),
        P(),
        P(),
        P(),
        P(),
        P(),
        P("row", "col"),
    )
    return jax.shard_map(
        on_device,
        mesh=mesh,
        in_specs=placed,
        out_specs=(P(("row", "col"), None), P("col", None), P(), P(), P()),
        check_vma=False,
    )
```

profile of v0, /device:TPU:1, one launch (start us, length us, event | category | flops | bytes accessed | tf_op | source)
XLA Modules:
  0.0 511.7 jit_solution(3659964022238284578)
XLA Ops:
  8.5 7.2 %all-to-all-start = ((bf16[16,2,6,128]{3,1,2,0:T(2,128)(2,1)}), bf16[16,2,6,128]{3,1,2,0:T(2,128)(2,1)S(1)}, u32[]{:S(2)}, u32[]{:S(2)}) async-start(bf16[16,2,6,128]{3,1,2,0:T(2,128)(2,1)} %broadcast_in_dim.22), calls=%async_computation | async-start | bytes 98304 | tf_op jit(solution)/shard_map/all_to_all | solution.py:9
  15.7 5.8 %all-to-all-done = bf16[16,2,6,128]{3,1,2,0:T(2,128)(2,1)S(1)} async-done(((bf16[16,2,6,128]{3,1,2,0:T(2,128)(2,1)}), bf16[16,2,6,128]{3,1,2,0:T(2,128)(2,1)S(1)}, u32[]{:S(2)}, u32[]{:S(2)}) %all-to-all-start) | async-done | bytes 49184 | tf_op jit(solution)/shard_map/all_to_all | solution.py:9
  21.8 45.1 %all_gather.3 = bf16[16,2,96,128]{3,2,1,0:T(8,128)(2,1)S(1)} all-gather(bf16[1,2,96,128]{3,2,1,0:T(8,128)(2,1)S(1)} %copy.34), channel_id=1, replica_groups=mesh['row'=16,'col'=16] {'row'}, dimensions={0}, use_global_device_ids=true | all-gather | bytes 835584 | tf_op jit(solution)/shard_map/all_gather | solution.py:26
  67.0 161.3 %while.19 = (s32[]{:T(128)}, f32[128,512]{1,0:T(8,128)S(1)}, f32[512,128]{1,0:T(8,128)S(1)}, f32[128,64]{0,1:T(8,128)S(1)}, f32[96,128]{1,0:T(8,128)S(1)}, /*ind...) while((s32[]{:T(128)}, f32[128,512]{1,0:T(8,128)S(1)}, ...), condition=%wide.region_11.12_spmd.clone, body=%wide.region_0.11_spmd.clone.sunk | while | flops 869032064 | bytes 20266860 | solution.py:131
  68.8 1.9 fusion.121
  71.5 1.6 multiply_convert_fusion.5
  74.1 1.5 fusion.122
  76.3 2.1 multiply_convert_fusion.6
  82.2 1.9 fusion.121
  84.9 1.6 multiply_convert_fusion.5
  89.8 2.1 multiply_convert_fusion.6
  95.7 1.9 fusion.121
  98.4 1.6 multiply_convert_fusion.5
  101.0 1.5 fusion.122
  103.2 2.1 multiply_convert_fusion.6
  109.1 1.9 fusion.121
  111.8 1.6 multiply_convert_fusion.5
  116.7 2.1 multiply_convert_fusion.6
  122.6 1.9 fusion.121
  125.3 1.6 multiply_convert_fusion.5
  130.1 2.1 multiply_convert_fusion.6
  136.0 1.9 fusion.121
  138.7 1.6 multiply_convert_fusion.5
  143.6 2.1 multiply_convert_fusion.6
  149.5 1.9 fusion.121
  152.2 1.6 multiply_convert_fusion.5
  157.0 2.1 multiply_convert_fusion.6
  162.9 1.9 fusion.121
  165.6 1.6 multiply_convert_fusion.5
  170.4 2.1 multiply_convert_fusion.6
  176.3 1.9 fusion.121
  179.1 1.6 multiply_convert_fusion.5
  183.9 2.1 multiply_convert_fusion.6
  189.8 1.9 fusion.121
  192.5 1.6 multiply_convert_fusion.5
  197.3 2.1 multiply_convert_fusion.6
  203.2 1.9 fusion.121
  205.9 1.6 multiply_convert_fusion.5
  210.8 2.1 multiply_convert_fusion.6
  216.7 1.9 fusion.121
  219.4 1.6 multiply_convert_fusion.5
  224.2 2.1 multiply_convert_fusion.6
  229.3 3.6 all-to-all-start.1
  234.3 64.3 %all-reduce = f32[96,128]{1,0:T(8,128)S(1)} all-reduce(f32[96,128]{1,0:T(8,128)S(1)} %bitcast.153), channel_id=2, replica_groups=mesh['row'=16,'col'=16] {'col'}, use_global_device_ids=true, to_apply=%region_12.13.clone | all-reduce | flops 12288 | bytes 98304
  299.1 77.9 %psum.23 = f32[128,64]{0,1:T(8,128)S(1)} all-reduce(f32[128,64]{0,1:T(8,128)S(1)} %get-tuple-element.95), channel_id=1, replica_groups=mesh['row'=16,'col'=16] {'row','col'}, use_global_device_ids=true, to_apply=%region_16.17 | all-reduce | flops 8192 | bytes 65536 | tf_op jit(solution)/shard_map/psum | solution.py:136
  377.7 123.2 %all-reduce.4.cloned.1.call-done = (f32[128,512]{1,0:T(8,128)}, f32[512,128]{1,0:T(8,128)}) async-done(((f32[128,512]{1,0:T(8,128)}, f32[512,128]{1,0:T(8,128)}), (f32[128,512]{1,0:T(8,128)}, f32[512,128]{1,0:T(8,128)})) %all-reduce.4.cloned.1.call-update) | async-done | bytes 524304 | tf_op jit(solution)/shard_map/psum | solution.py:136
  500.8 1.7 broadcast_multiply_fusion.5
  502.5 1.7 broadcast_multiply_fusion.4
  (589 shorter events, 92.5 us)
Async XLA Ops:
  8.5 13.0 %all-to-all-start = ((bf16[16,2,6,128]{3,1,2,0:T(2,128)(2,1)}), bf16[16,2,6,128]{3,1,2,0:T(2,128)(2,1)S(1)}, u32[]{:S(2)}, u32[]{:S(2)}) async-start(bf16[16,2,6,128]{3,1,2,0:T(2,128)(2,1)} %broadcast_in_dim.22), calls=%async_computation | async-start | bytes 98304 | tf_op jit(solution)/shard_map/all_to_all | solution.py:9
  68.7 2.4 copy-start.5
  68.8 2.4 copy-start.6
  68.8 2.7 copy-start.2
  68.8 2.7 copy-start.7
  82.2 2.4 copy-start.5
  82.2 2.7 copy-start.2
  82.2 2.7 copy-start.7
  95.6 2.4 copy-start.5
  95.6 2.4 copy-start.6
  95.7 2.7 copy-start.2
  95.7 2.7 copy-start.7
  109.1 2.4 copy-start.5
  109.1 2.7 copy-start.2
  109.1 2.7 copy-start.7
  122.5 2.4 copy-start.5
  122.5 2.4 copy-start.6
  122.5 2.7 copy-start.2
  122.6 2.7 copy-start.7
  136.0 2.4 copy-start.5
  136.0 2.7 copy-start.2
  136.0 2.7 copy-start.7
  149.4 2.4 copy-start.5
  149.4 2.4 copy-start.6
  149.4 2.7 copy-start.2
  149.4 2.7 copy-start.7
  162.9 2.4 copy-start.5
  162.9 2.7 copy-start.2
  162.9 2.7 copy-start.7
  176.3 2.4 copy-start.5
  176.3 2.4 copy-start.6
  176.3 2.7 copy-start.2
  176.3 2.7 copy-start.7
  189.7 2.4 copy-start.5
  189.8 2.7 copy-start.2
  189.8 2.7 copy-start.7
  203.2 2.4 copy-start.5
  203.2 2.4 copy-start.6
  203.2 2.7 copy-start.2
  203.2 2.7 copy-start.7
  216.6 2.4 copy-start.5
  216.7 2.7 copy-start.2
  216.7 2.7 copy-start.7
  228.3 6.0 %copy-start = (f32[512,128]{1,0:T(8,128)}, f32[512,128]{1,0:T(8,128)S(1)}, u32[]{:S(2)}) copy-start(f32[512,128]{1,0:T(8,128)S(1)} %get-tuple-element.94) | copy-start | bytes 786436
  228.3 6.0 %copy-start.1 = (f32[128,512]{1,0:T(8,128)}, f32[128,512]{1,0:T(8,128)S(1)}, u32[]{:S(2)}) copy-start(f32[128,512]{1,0:T(8,128)S(1)} %get-tuple-element.93) | copy-start | bytes 786436
  228.3 4.7 copy-start.8
  229.3 274.9 %all-to-all-start.1 = ((f32[16,96,128]{2,1,0:T(8,128)}), f32[16,96,128]{2,1,0:T(8,128)S(1)}, u32[]{:S(2)}, u32[]{:S(2)}) async-start(f32[16,96,128]{2,1,0:T(8,128)} %broadcast_in_dim.23), calls=%async_computation.1 | async-start | bytes 1572864 | tf_op jit(solution)/shard_map/all_to_all | solution.py:9
  232.9 267.9 %all-reduce.4.cloned.1.call-start = ((), (), s32[]{:S(2)}) async-start(), calls=%async_computation.2 | async-start | bytes 1048576 | tf_op jit(solution)/shard_map/psum | solution.py:136
  (30 other events, 58.8 us)
Sparse Core Ops, SparseCore 0:
  240.0 260.8 all-reduce.3
where the time goes:
time: 514 us; the launch traced here: 512 us
  blocking collectives  187 us (36%)
  waiting for transfers between devices  129 us (25%)
  matrix products  113 us (22%)
  other arithmetic  28 us (5%)
  local copies, waits for them, and re-layouts  25.2 us (5%)
  between operations  14.8 us (3%)
  starting transfers between devices  10.8 us (2%)
    psum x1, waiting for transfers between devices, on_device(): lax.psum((running[0], running[1], running[2]), ('row', 'col'))  123 us
    psum x1, blocking collectives, on_device(): lax.psum((running[0], running[1], running[2]), ('row', 'col'))  77.9 us
    unnamed x1, blocking collectives  64.3 us
    all_gather x1, blocking collectives, picked(): lax.all_gather(value, axis)  45.1 us
    dot_general x36, matrix products, outer(): lax.dot_general(first, second, (((1,), (1,)), ((), ())), preferred_elemen...  34.7 us
    dot_general x24, matrix products, transition(): jnp.dot(hidden, w_out, preferred_element_type=jnp.float32)  27.4 us
    dot_general x12, matrix products, transition(): pre_act = jnp.dot(normed, w_in, preferred_element_type=jnp.float32) + b_in  19.6 us
    div x12, matrix products, pair_backward(): probs = expo / jnp.sum(expo, axis=-1, keepdims=True)  17.9 us
  transfers between devices with their start and end apart: 3, of which 2 were waited for; matrix products, arithmetic and copies ran while one was open for 1% of the time, Pallas kernels for 0%

commit v1 on v0

v1 whole, which is shorter than its diff:
```python
import functools

import jax
import jax.numpy as jnp
from jax import lax
from jax.experimental import pallas as pl
from jax.experimental.pallas import tpu as pltpu
from jax.sharding import PartitionSpec as P

GROUP = 8
F32 = jnp.float32
BF16 = jnp.bfloat16


def from_everyone(value, axis):
    count = lax.axis_size(axis)
    return lax.all_to_all(
        jnp.broadcast_to(value[None], (count, *value.shape)), axis, 0, 0, tiled=True
    )


def inner(first, second):
    return lax.dot_general(first, second, (((0,), (0,)), ((), ())), preferred_element_type=F32)


def dot(first, second):
    return jnp.dot(first, second, preferred_element_type=F32)


def pair_kernel(
    place,
    from_row_mates,
    from_col_mates,
    gain_ref,
    bias_ref,
    w_in_ref,
    b_in_ref,
    w_out_ref,
    w_bins_ref,
    w_in_t_ref,
    w_out_t_ref,
    w_bins_t_ref,
    col_out,
    row_out,
    own_out,
    blk,
    blk_center,
    far_side,
    far_center,
    label_rows,
    grad_in,
    grad_out_t,
    grad_bins,
    blk_sums,
    side_sums,
    *,
    count,
    rows,
):
    block = count * rows
    half = block // 2
    width = gain_ref.shape[1]
    row_at = place[0]
    col_at = place[1]

    for m in range(count):
        for side in range(2):
            blk[side, m * rows : (m + 1) * rows, :] = from_row_mates[
                m, rows * (1 + side) : rows * (2 + side), :
            ]
    far_side[...] = jnp.zeros_like(far_side)
    label_rows[...] = jnp.zeros_like(label_rows)
    for m in range(count // 2 + 1):
        source = lax.rem(row_at + m, count)
        for side in range(2):
            far_side[side, m * rows : (m + 1) * rows, :] = from_col_mates[
                source, rows * side : rows * (side + 1), :
            ]
        label_rows[m * rows : (m + 1) * rows, :] = from_row_mates[source, 0:rows, :]
    if rows < GROUP:
        for side in range(2):
            far_side[side, half + rows : half + GROUP, :] = far_side[side, rows:GROUP, :]
        label_rows[half + rows : half + GROUP, :] = label_rows[rows:GROUP, :]
    for side in range(2):
        value = blk[side]
        blk_center[side] = value - jnp.mean(value, axis=-1, keepdims=True)
        value = far_side[side]
        far_center[side] = value - jnp.mean(value, axis=-1, keepdims=True)

    grad_in[...] = jnp.zeros_like(grad_in)
    grad_out_t[...] = jnp.zeros_like(grad_out_t)
    grad_bins[...] = jnp.zeros_like(grad_bins)
    side_sums[...] = jnp.zeros_like(side_sums)

    gain = gain_ref[...]
    bias = bias_ref[...]
    sub = lax.broadcasted_iota(jnp.int32, (GROUP, width), 0)
    lane = lax.broadcasted_iota(jnp.int32, (GROUP, width), 1)
    bin_lane = lax.broadcasted_iota(jnp.int32, (GROUP, w_bins_ref.shape[1]), 1).astype(F32)
    own_at = rows * col_at + sub
    span = GROUP * half
    every = span + GROUP

    apart_label = jnp.sum(
        jnp.where(lane == own_at, label_rows[half : half + GROUP, :], 0.0), axis=-1, keepdims=True
    )

    def step(s, carry):
        first = pl.multiple_of(s * GROUP, GROUP)
        eight = [blk[side, pl.ds(first, GROUP), :] for side in range(2)]
        eight_center = [blk_center[side, pl.ds(first, GROUP), :] for side in range(2)]
        near = [(sub >= rows) | (own_at >= first + ii) for ii in range(GROUP)]

        def listed(ref, mask, *lead):
            head = jnp.where(
                mask, ref[(*lead, slice(0, GROUP))], ref[(*lead, slice(half, half + GROUP))]
            )
            return head

        summed, center = [], []
        for side in range(2):
            for ii in range(GROUP):
                for source, own, into in (
                    (far_side, eight, summed),
                    (far_center, eight_center, center),
                ):
                    one = own[side][ii : ii + 1, :]
                    into.append(listed(source, near[ii], 1 - side) + one)
                    if half > GROUP:
                        into.append(source[1 - side, GROUP:half, :] + one)
            for source, into in ((far_side, summed), (far_center, center)):
                into.append(source[side, 0:GROUP, :] + source[1 - side, half : half + GROUP, :])
        summed = jnp.concatenate(summed, axis=0)
        center = jnp.concatenate(center, axis=0)
        inv_scale = lax.rsqrt(jnp.mean(center * center, axis=-1, keepdims=True) + 1e-05)
        normal_form = center * inv_scale
        normed = (normal_form * gain + bias).astype(BF16)
        act = dot(normed, w_in_ref[...]) + b_in_ref[...]
        up = jnp.tanh(act) + 1.0
        hidden = (act * up).astype(BF16)
        slope = up * (act * (2.0 - up) + 1.0)
        updated = (summed + dot(hidden, w_out_ref[...])).astype(BF16)
        logits = dot(updated, w_bins_ref[...])
        sym = logits[0:every] + logits[every:]

        hots, scales = [], []
        rest = jnp.full((half - GROUP, 1), 2.0, F32) if half > GROUP else None
        for ii in range(GROUP):
            picked = []
            for lo, hi in ((0, GROUP), (half, half + GROUP)):
                picked.append(
                    jnp.sum(
                        jnp.where(lane == first + ii, label_rows[lo:hi, :], 0.0),
                        axis=-1,
                        keepdims=True,
                    )
                )
            hots.append(jnp.where(near[ii][:, 0:1], picked[0], picked[1]))
            own = (own_at[:, 0:1] == first + ii) & (sub[:, 0:1] < rows)
            scales.append(jnp.where(own, 1.0, 2.0))
            if half > GROUP:
                wide = lax.broadcasted_iota(jnp.int32, (half - GROUP, width), 1)
                hots.append(
                    jnp.sum(
                        jnp.where(wide == first + ii, label_rows[GROUP:half, :], 0.0),
                        axis=-1,
                        keepdims=True,
                    )
                )
                scales.append(rest)
        hots.append(apart_label)
        scales.append(jnp.where((sub[:, 0:1] < rows) & (s == 0), 1.0, 0.0))
        hot = jnp.concatenate(hots, axis=0)
        scale = jnp.concatenate(scales, axis=0)
        lanes = jnp.broadcast_to(bin_lane[0:1], sym.shape)
        expo = jnp.exp(sym - jnp.max(sym, axis=-1, keepdims=True))
        probs = expo / jnp.sum(expo, axis=-1, keepdims=True)
        logit_grad = (scale * (probs - jnp.where(lanes == hot, 1.0, 0.0))).astype(BF16)

        upd_grad = dot(logit_grad, w_bins_t_ref[...])
        upd_half = upd_grad.astype(BF16)
        grad_bins[...] += inner(updated[0:every], logit_grad) + inner(updated[every:], logit_grad)
        grad_out_t[...] += inner(upd_half, hidden[0:every]) + inner(upd_half, hidden[every:])
        hid_grad = dot(upd_half, w_out_t_ref[...])
        pre_grad = jnp.concatenate(
            [(hid_grad * slope[0:every]).astype(BF16), (hid_grad * slope[every:]).astype(BF16)],
            axis=0,
        )
        grad_in[...] += inner(normed, pre_grad)
        norm_grad = dot(pre_grad, w_in_t_ref[...]) * gain
        pair_grad = inv_scale * (
            norm_grad
            - jnp.mean(norm_grad, axis=-1, keepdims=True)
            - normal_form * jnp.mean(norm_grad * normal_form, axis=-1, keepdims=True)
        )
        for side in range(2):
            mine = pair_grad[side * every : (side + 1) * every] + upd_grad
            ones, head_near, head_far, tail = [], None, None, None
            for ii in range(GROUP):
                part = mine[ii * half : (ii + 1) * half]
                ones.append(jnp.sum(part, axis=0, keepdims=True))
                close = jnp.where(near[ii], part[0:GROUP], 0.0)
                away = part[0:GROUP] - close
                head_near = close if ii == 0 else head_near + close
                head_far = away if ii == 0 else head_far + away
                if half > GROUP:
                    tail = part[GROUP:] if ii == 0 else tail + part[GROUP:]
            blk_sums[side, pl.ds(first, GROUP), :] = jnp.concatenate(ones, axis=0)
            side_sums[1 - side, 0:GROUP, :] += head_near
            side_sums[1 - side, half : half + GROUP, :] += head_far
            if half > GROUP:
                side_sums[1 - side, GROUP:half, :] += tail
            side_sums[side, half + GROUP : half + 2 * GROUP, :] += mine[span:]
            side_sums[1 - side, half : half + GROUP, :] += mine[span:]
        return carry

    lax.fori_loop(0, block // GROUP, step, 0)

    share_in = grad_in.shape[0] // count
    share_out = grad_out_t.shape[1] // count
    tiles = grad_in.shape[1] // width
    grad_out = grad_out_t[...].T
    bins = grad_bins[...]
    bins = jnp.concatenate([bins, jnp.zeros_like(bins)], axis=1)
    for m in range(count):
        at = 0
        for t in range(tiles):
            col_out[m, at : at + share_in, :] = grad_in[
                m * share_in : (m + 1) * share_in, t * width : (t + 1) * width
            ]
            at += share_in
        col_out[m, at : at + share_out, :] = grad_out[m * share_out : (m + 1) * share_out]
        at += share_out
        col_out[m, at : at + share_in, :] = bins[m * share_in : (m + 1) * share_in]
        at += share_in
        for side in range(2):
            col_out[m, at : at + GROUP, :] = jnp.zeros((GROUP, width), F32)
            col_out[m, at : at + rows, :] = blk_sums[side, m * rows : (m + 1) * rows, :]
            at += GROUP
    row_out[...] = jnp.zeros_like(row_out)
    for m in range(count // 2 + 1):
        target = lax.rem(row_at + m, count)
        for side in range(2):
            row_out[target, side * GROUP : side * GROUP + rows, :] = side_sums[
                side, m * rows : (m + 1) * rows, :
            ]
    for side in range(2):
        own_out[side * GROUP : (side + 1) * GROUP, :] = side_sums[
            side, half + GROUP : half + 2 * GROUP, :
        ]


def run_pairs(place, from_row_mates, from_col_mates, gain, bias, w_in, b_in, w_out, w_bins):
    count = from_row_mates.shape[0]
    rows = from_row_mates.shape[1] // 3
    width, hidden = w_in.shape
    bins = w_bins.shape[1]
    block = count * rows
    half = block // 2
    share = (width // count) * (hidden // width) + hidden // count + width // count
    vmem = pl.BlockSpec(memory_space=pltpu.VMEM)
    smem = pl.BlockSpec(memory_space=pltpu.SMEM)
    halved = w_in * jnp.asarray(0.5, BF16)
    return pl.pallas_call(
        functools.partial(pair_kernel, count=count, rows=rows),
        out_shape=(
            jax.ShapeDtypeStruct((count, share + 2 * GROUP, width), F32),
            jax.ShapeDtypeStruct((count, 2 * GROUP, width), F32),
            jax.ShapeDtypeStruct((2 * GROUP, width), F32),
        ),
        in_specs=[smem] + [vmem] * 11,
        out_specs=(vmem, vmem, vmem),
        scratch_shapes=[
            pltpu.VMEM((2, block, width), F32),
            pltpu.VMEM((2, block, width), F32),
            pltpu.VMEM((2, half + GROUP, width), F32),
            pltpu.VMEM((2, half + GROUP, width), F32),
            pltpu.VMEM((half + GROUP, width), F32),
            pltpu.VMEM((width, hidden), F32),
            pltpu.VMEM((width, hidden), F32),
            pltpu.VMEM((width, bins), F32),
            pltpu.VMEM((2, block, width), F32),
            pltpu.VMEM((2, half + 2 * GROUP, width), F32),
        ],
        compiler_params=pltpu.CompilerParams(vmem_limit_bytes=56 * 1024 * 1024),
        interpret=INTERPRET,
        name="pairs",
    )(
        place,
        from_row_mates.astype(F32),
        from_col_mates.astype(F32),
        gain[None],
        bias[None],
        halved,
        0.5 * b_in[None],
        w_out,
        w_bins,
        w_in.T,
        w_out.T * jnp.asarray(0.5, BF16),
        w_bins.T,
    )


INTERPRET = False


def on_device(left_act, right_act, norm_gain, norm_bias, w_in, b_in, w_out, w_bins, labels):
    count = lax.axis_size("col")
    rows, width = left_act.shape
    hidden = w_in.shape[1]
    row_at = lax.axis_index("row")
    col_at = lax.axis_index("col")
    stacked = jnp.concatenate([left_act, right_act], axis=0)
    turned = jnp.pad(labels.T.astype(BF16), ((0, 0), (0, width - labels.shape[0])))
    to_row_mates = jnp.concatenate(
        [
            turned.reshape(count, rows, width),
            jnp.broadcast_to(stacked[None], (count, 2 * rows, width)),
        ],
        axis=1,
    )
    from_row_mates = lax.all_to_all(to_row_mates, "col", 0, 0, tiled=True)
    from_col_mates = from_everyone(stacked, "row")
    place = jnp.stack([row_at, col_at]).astype(jnp.int32)
    col_out, row_out, own_out = run_pairs(
        place, from_row_mates, from_col_mates, norm_gain, norm_bias, w_in, b_in, w_out, w_bins
    )
    by_col = lax.all_to_all(col_out, "col", 0, 0, tiled=True).sum(axis=0)
    by_row = lax.all_to_all(row_out, "row", 0, 0, tiled=True).sum(axis=0)
    share = by_col.shape[0] - 2 * GROUP
    both = by_col[share:] + by_row + own_out
    grad_left = both[0:rows]
    size = lax.axis_size("row")
    swap = [(a * count + b, b * count + a) for a in range(size) for b in range(count)]
    right = lax.ppermute(both[GROUP:], ("row", "col"), swap)
    weights = from_everyone(by_col[0:share], "row").sum(axis=0) / (rows * count * size)
    grad_right = from_everyone(right, "row")[:, 0:rows].reshape(rows * size, width)
    weights = from_everyone(weights, "col")
    cut = (width // count) * (hidden // width)
    grad_in = (
        weights[:, 0:cut]
        .reshape(count, hidden // width, width // count, width)
        .transpose(0, 2, 1, 3)
        .reshape(width, hidden)
    )
    grad_out = weights[:, cut : cut + hidden // count].reshape(hidden, width)
    grad_bins = weights[:, cut + hidden // count :, 0 : w_bins.shape[1]].reshape(width, -1)
    return (grad_left, grad_right, grad_in, grad_out, grad_bins)


def solution(mesh):
    placed = (
        P(("row", "col"), None),
        P(("row", "col"), None),
        P(),
        P(),
        P(),
        P(),
        P(),
        P(),
        P("row", "col"),
    )
    return jax.shard_map(
        on_device,
        mesh=mesh,
        in_specs=placed,
        out_specs=(P(("row", "col"), None), P("col", None), P(), P(), P()),
        check_vma=False,
    )
```

time: 514 us -> 162 us (0.32)
  blocking collectives: 187 us -> 16.2 us
  matrix products: 113 us -> 0 us
  waiting for transfers between devices: 129 us -> 47.2 us
  Pallas kernels: 0 us -> 36.1 us
  starting transfers between devices: 10.8 us -> 44.8 us
  other arithmetic: 28 us -> 6.27 us
  local copies, waits for them, and re-layouts: 25.2 us -> 9.19 us
  between operations: 14.8 us -> 0.79 us
    psum x1 -> x0, waiting for transfers between devices: 123 us -> none  [on_device(): lax.psum((running[0], running[1], running[2]), ('row', 'col'))]
    dot_general x120 -> x0, matrix products: 95.4 us -> none  [the longest x36 34.7 us: outer(): lax.dot_general(first, second, (((1,), (1,)), ((), ())), preferred_elemen...]
    psum x1 -> x0, blocking collectives: 77.9 us -> none  [on_device(): lax.psum((running[0], running[1], running[2]), ('row', 'col'))]
    unnamed x1 -> x0, blocking collectives: 64.3 us -> none
    all_gather x1 -> x0, blocking collectives: 45.1 us -> none  [picked(): lax.all_gather(value, axis)]
    pallas_call x0 -> x1, Pallas kernels: none -> 36.1 us  [run_pairs(): pl.pallas_call(functools.partial(pair_kernel, count=count, rows=rows), ou...]
    all_to_all x2 -> x4, waiting for transfers between devices: 5.77 us -> 25 us  [from_everyone(): lax.all_to_all(jnp.broadcast_to(value[None], (count, *value.shape)), axis...]
    all_to_all x2 -> x4, starting transfers between devices: 10.8 us -> 28.7 us  [from_everyone(): lax.all_to_all(jnp.broadcast_to(value[None], (count, *value.shape)), axis...]
  transfers between devices with their start and end apart: 3 -> 7, of which waited for: 2 -> 7; matrix products, arithmetic and copies ran while one was open for 1% -> 5% of each run, Pallas kernels for 0% -> 0%
where the time goes in v1:
time: 162 us; the launch traced here: 161 us
  waiting for transfers between devices  47.2 us (29%)
  starting transfers between devices  44.8 us (28%)
  Pallas kernels  36.1 us (22%)
  blocking collectives  16.2 us (10%)
  local copies, waits for them, and re-layouts  9.19 us (6%)
  other arithmetic  6.27 us (4%)
    pallas_call x1, Pallas kernels, run_pairs(): pl.pallas_call(functools.partial(pair_kernel, count=count, rows=rows), ou...  36.1 us
    all_to_all x4, starting transfers between devices, from_everyone(): lax.all_to_all(jnp.broadcast_to(value[None], (count, *value.shape)), axis...  28.7 us
    all_to_all x4, waiting for transfers between devices, from_everyone(): lax.all_to_all(jnp.broadcast_to(value[None], (count, *value.shape)), axis...  25 us
    all_to_all x1, blocking collectives, on_device(): by_col = lax.all_to_all(col_out, 'col', 0, 0, tiled=True).sum(axis=0)  16.2 us
    all_to_all x1, waiting for transfers between devices, on_device(): by_row = lax.all_to_all(row_out, 'row', 0, 0, tiled=True).sum(axis=0)  10.2 us
    ppermute x1, waiting for transfers between devices, on_device(): right = lax.ppermute(both[GROUP:], ('row', 'col'), swap)  9.6 us
    all_to_all x1, starting transfers between devices, on_device(): from_row_mates = lax.all_to_all(to_row_mates, 'col', 0, 0, tiled=True)  6.92 us
    ppermute x1, starting transfers between devices, on_device(): right = lax.ppermute(both[GROUP:], ('row', 'col'), swap)  5.6 us
  transfers between devices with their start and end apart: 7, of which 7 were waited for; matrix products, arithmetic and copies ran while one was open for 5% of the time, Pallas kernels for 0%

profile of v1, /device:TPU:1, one launch (start us, length us, event | category | flops | bytes accessed | tf_op | source)
XLA Modules:
  0.0 160.6 jit_solution(14707475884096768960)
XLA Ops:
  0.6 0.7 pad_maximum_fusion.1
  1.3 0.6 broadcast_in_dim.12
  2.0 0.0 copy-start.3
  2.0 11.9 %all-to-all-start.1 = ((bf16[16,12,128]{2,1,0:T(8,128)(2,1)}), bf16[16,12,128]{2,1,0:T(8,128)(2,1)S(1)}, u32[]{:S(2)}, u32[]{:S(2)}) async-start(bf16[16,12,128]{2,1,0:T(8,128)(2,1)} %broadcast_in_dim.12), calls=%async_computation.1 | async-start | bytes 131072 | tf_op jit(solution)/shard_map/all_to_all | solution.py:17
  13.9 0.0 copy-done.3
  13.9 0.0 copy-start
  13.9 0.1 copy.30
  14.0 0.7 copy-done
  14.8 0.0 copy-start.1
  14.8 0.7 broadcast_multiply_fusion.w_in_ref
  15.4 0.3 copy-done.1
  15.7 0.1 copy.27
  15.8 0.7 multiply_bitcast_fusion.w_out_t_ref
  16.5 1.5 pad_maximum_fusion
  18.0 0.0 copy-start.5
  18.0 4.8 %all-to-all-done.1 = bf16[16,12,128]{2,1,0:T(8,128)(2,1)S(1)} async-done(((bf16[16,12,128]{2,1,0:T(8,128)(2,1)}), bf16[16,12,128]{2,1,0:T(8,128)(2,1)S(1)}, u32[]{:S(2)}, u32[]{:S(2)}) %all-to-all-start.1) | async-done | bytes 49184 | tf_op jit(solution)/shard_map/all_to_all | solution.py:17
  22.9 6.9 %all-to-all-start = ((bf16[16,18,128]{2,1,0:T(8,128)(2,1)}), bf16[16,18,128]{2,1,0:T(8,128)(2,1)S(1)}, u32[]{:S(2)}, u32[]{:S(2)}) async-start(bf16[16,18,128]{2,1,0:T(8,128)(2,1)} %pad_maximum_fusion), calls=%async_computation | async-start | bytes 196608 | tf_op jit(solution)/shard_map/all_to_all | solution.py:322
  29.8 0.0 copy-done.5
  29.8 0.6 broadcast_multiply_fusion.2
  30.4 0.0 copy-start.2
  30.4 0.8 copy.26
  31.1 0.0 copy-done.2
  31.1 0.7 copy.28.w_bins_ref
  31.9 0.7 pad_add_fusion.place
  32.5 0.7 convert_element_type.17.from_col_mates
  33.2 2.5 %all-to-all-done = bf16[16,18,128]{2,1,0:T(8,128)(2,1)S(1)} async-done(((bf16[16,18,128]{2,1,0:T(8,128)(2,1)}), bf16[16,18,128]{2,1,0:T(8,128)(2,1)S(1)}, u32[]{:S(2)}, u32[]{:S(2)}) %all-to-all-start) | async-done | bytes 73760 | tf_op jit(solution)/shard_map/all_to_all | solution.py:322
  35.6 0.7 convert_element_type.16.from_row_mates
  36.3 36.1 %pairs.1 = (f32[16,88,128]{2,1,0:T(8,128)}, f32[16,16,128]{2,1,0:T(8,128)}, f32[16,128]{1,0:T(8,128)}) custom-call(s32[2]{0:T(128)} %pad_add_fusion.place, f32[16,18,128]{2,1,0:T(8,128)} %convert_element_type.16.from_row_mates, f32[16,12,128]{2,1,0:T(8,128)} %convert_element_type.17.from_col_mates, f32[1,128]{1,0:T(1,128)} %bitcast.26, f32[1,128]{1,0:T(1,128)} %bitcast.27, ...), custom_call_target="tpu_custom_call" | custom-call | tf_op jit(solution)/shard_map/pairs/pallas_call | solution.py:264
  72.5 16.2 %all_to_all.35 = f32[16,88,128]{2,1,0:T(8,128)S(1)} all-to-all(f32[16,88,128]{2,1,0:T(8,128)} %get-tuple-element.8), channel_id=1, replica_groups=mesh['row'=16,'col'=16] {'col'}, dimensions={0} | all-to-all | bytes 1441792 | tf_op jit(solution)/shard_map/all_to_all | solution.py:328
  88.7 3.5 %all-to-all-start.3 = ((f32[16,16,128]{2,1,0:T(8,128)}), f32[16,16,128]{2,1,0:T(8,128)S(1)}, u32[]{:S(2)}, u32[]{:S(2)}) async-start(f32[16,16,128]{2,1,0:T(8,128)} %get-tuple-element.9), calls=%async_computation.3 | async-start | bytes 262144 | tf_op jit(solution)/shard_map/all_to_all | solution.py:329
  92.3 10.2 %all-to-all-done.3 = f32[16,16,128]{2,1,0:T(8,128)S(1)} async-done(((f32[16,16,128]{2,1,0:T(8,128)}), f32[16,16,128]{2,1,0:T(8,128)S(1)}, u32[]{:S(2)}, u32[]{:S(2)}) %all-to-all-start.3) | async-done | bytes 131104 | tf_op jit(solution)/shard_map/all_to_all | solution.py:329
  102.5 0.9 broadcast_in_dim.16
  103.4 3.6 %all-to-all-start.5 = ((f32[16,72,128]{2,1,0:T(8,128)}), f32[16,72,128]{2,1,0:T(8,128)S(1)}, u32[]{:S(2)}, u32[]{:S(2)}) async-start(f32[16,72,128]{2,1,0:T(8,128)} %broadcast_in_dim.16), calls=%async_computation.5 | async-start | bytes 1179648 | tf_op jit(solution)/shard_map/all_to_all | solution.py:17
  107.0 0.0 copy-start.4
  107.0 0.7 copy-done.4
  107.7 5.6 %collective-permute-start = (f32[8,128]{1,0:T(8,128)S(1)}, f32[8,128]{1,0:T(8,128)S(1)}, u32[]{:S(2)}, u32[]{:S(2)}) collective-permute-start(f32[8,128]{1,0:T(8,128)S(1)} %slice.34), channel_id=1, source_target_pairs={{0,0},{1,16},{2,32},{3,48},{4,64},{5,80},{6,96},{7,112},{8,128},{9... | collective-permute-start | bytes 12296 | tf_op jit(solution)/shard_map/ppermute | solution.py:335
  113.3 9.6 %collective-permute-done = f32[8,128]{1,0:T(8,128)S(1)} collective-permute-done((f32[8,128]{1,0:T(8,128)S(1)}, f32[8,128]{1,0:T(8,128)S(1)}, u32[]{:S(2)}, u32[]{:S(2)}) %collective-permute-start) | collective-permute-done | bytes 4128 | tf_op jit(solution)/shard_map/ppermute | solution.py:335
  122.9 2.0 %all-to-all-done.5 = f32[16,72,128]{2,1,0:T(8,128)S(1)} async-done(((f32[16,72,128]{2,1,0:T(8,128)}), f32[16,72,128]{2,1,0:T(8,128)S(1)}, u32[]{:S(2)}, u32[]{:S(2)}) %all-to-all-start.5) | async-done | bytes 589856 | tf_op jit(solution)/shard_map/all_to_all | solution.py:17
  124.8 0.6 broadcast_in_dim.15
  125.5 5.7 %all-to-all-start.4 = ((f32[16,8,128]{2,1,0:T(8,128)}), f32[16,8,128]{2,1,0:T(8,128)S(1)}, u32[]{:S(2)}, u32[]{:S(2)}) async-start(f32[16,8,128]{2,1,0:T(8,128)} %broadcast_in_dim.15), calls=%async_computation.4 | async-start | bytes 131072 | tf_op jit(solution)/shard_map/all_to_all | solution.py:17
  131.3 9.0 %all-to-all-done.4 = f32[16,8,128]{2,1,0:T(8,128)S(1)} async-done(((f32[16,8,128]{2,1,0:T(8,128)}), f32[16,8,128]{2,1,0:T(8,128)S(1)}, u32[]{:S(2)}, u32[]{:S(2)}) %all-to-all-start.4) | async-done | bytes 65568 | tf_op jit(solution)/shard_map/all_to_all | solution.py:17
  140.2 0.9 broadcast_in_dim.17
  141.1 7.5 %all-to-all-start.6 = ((f32[16,72,128]{2,1,0:T(8,128)}), f32[16,72,128]{2,1,0:T(8,128)S(1)}, u32[]{:S(2)}, u32[]{:S(2)}) async-start(f32[16,72,128]{2,1,0:T(8,128)} %broadcast_in_dim.17), calls=%async_computation.6 | async-start | bytes 1179648 | tf_op jit(solution)/shard_map/all_to_all | solution.py:17
  148.6 0.6 slice.33
  149.2 0.6 reshape.36
  149.9 9.2 %all-to-all-done.6 = f32[16,72,128]{2,1,0:T(8,128)S(1)} async-done(((f32[16,72,128]{2,1,0:T(8,128)}), f32[16,72,128]{2,1,0:T(8,128)S(1)}, u32[]{:S(2)}, u32[]{:S(2)}) %all-to-all-start.6) | async-done | bytes 589856 | tf_op jit(solution)/shard_map/all_to_all | solution.py:17
  159.1 0.7 copy.29
  159.8 0.8 fusion.1
  (11 shorter events, 0.2 us)
Async XLA Ops:
  2.0 11.9 %copy-start.3 = (s32[96,96]{1,0:T(8,128)S(1)}, s32[96,96]{1,0:T(8,128)}, u32[]{:S(2)}) copy-start(s32[96,96]{1,0:T(8,128)} %param.17) | copy-start | bytes 110596
  2.0 20.9 %all-to-all-start.1 = ((bf16[16,12,128]{2,1,0:T(8,128)(2,1)}), bf16[16,12,128]{2,1,0:T(8,128)(2,1)S(1)}, u32[]{:S(2)}, u32[]{:S(2)}) async-start(bf16[16,12,128]{2,1,0:T(8,128)(2,1)} %broadcast_in_dim.12), calls=%async_computation.1 | async-start | bytes 131072 | tf_op jit(solution)/shard_map/all_to_all | solution.py:17
  13.9 0.9 copy-start
  14.8 1.0 copy-start.1
  18.0 11.8 %copy-start.5 = (f32[512]{0:T(512)S(1)}, f32[512]{0:T(512)}, u32[]{:S(2)}) copy-start(f32[512]{0:T(512)} %param.14) | copy-start | bytes 6148
  22.9 12.8 %all-to-all-start = ((bf16[16,18,128]{2,1,0:T(8,128)(2,1)}), bf16[16,18,128]{2,1,0:T(8,128)(2,1)S(1)}, u32[]{:S(2)}, u32[]{:S(2)}) async-start(bf16[16,18,128]{2,1,0:T(8,128)(2,1)} %pad_maximum_fusion), calls=%async_computation | async-start | bytes 196608 | tf_op jit(solution)/shard_map/all_to_all | solution.py:322
  30.4 0.8 copy-start.2
  88.7 13.8 %all-to-all-start.3 = ((f32[16,16,128]{2,1,0:T(8,128)}), f32[16,16,128]{2,1,0:T(8,128)S(1)}, u32[]{:S(2)}, u32[]{:S(2)}) async-start(f32[16,16,128]{2,1,0:T(8,128)} %get-tuple-element.9), calls=%async_computation.3 | async-start | bytes 262144 | tf_op jit(solution)/shard_map/all_to_all | solution.py:329
  103.4 21.5 %all-to-all-start.5 = ((f32[16,72,128]{2,1,0:T(8,128)}), f32[16,72,128]{2,1,0:T(8,128)S(1)}, u32[]{:S(2)}, u32[]{:S(2)}) async-start(f32[16,72,128]{2,1,0:T(8,128)} %broadcast_in_dim.16), calls=%async_computation.5 | async-start | bytes 1179648 | tf_op jit(solution)/shard_map/all_to_all | solution.py:17
  107.0 0.7 copy-start.4
  107.7 15.2 %collective-permute-start = (f32[8,128]{1,0:T(8,128)S(1)}, f32[8,128]{1,0:T(8,128)S(1)}, u32[]{:S(2)}, u32[]{:S(2)}) collective-permute-start(f32[8,128]{1,0:T(8,128)S(1)} %slice.34), channel_id=1, source_target_pairs={{0,0},{1,16},{2,32},{3,48},{4,64},{5,80},{6,96},{7,112},{8,128},{9... | collective-permute-start | bytes 12296 | tf_op jit(solution)/shard_map/ppermute | solution.py:335
  125.5 14.8 %all-to-all-start.4 = ((f32[16,8,128]{2,1,0:T(8,128)}), f32[16,8,128]{2,1,0:T(8,128)S(1)}, u32[]{:S(2)}, u32[]{:S(2)}) async-start(f32[16,8,128]{2,1,0:T(8,128)} %broadcast_in_dim.15), calls=%async_computation.4 | async-start | bytes 131072 | tf_op jit(solution)/shard_map/all_to_all | solution.py:17
  141.1 17.9 %all-to-all-start.6 = ((f32[16,72,128]{2,1,0:T(8,128)}), f32[16,72,128]{2,1,0:T(8,128)S(1)}, u32[]{:S(2)}, u32[]{:S(2)}) async-start(f32[16,72,128]{2,1,0:T(8,128)} %broadcast_in_dim.17), calls=%async_computation.6 | async-start | bytes 1179648 | tf_op jit(solution)/shard_map/all_to_all | solution.py:17

commit v2 on v1

v2 whole, which is shorter than its diff:
```python
import functools

import jax
import jax.numpy as jnp
from jax import lax
from jax.experimental import pallas as pl
from jax.experimental.pallas import tpu as pltpu
from jax.sharding import PartitionSpec as P

GROUP = 8
F32 = jnp.float32
BF16 = jnp.bfloat16


def from_everyone(value, axis):
    count = lax.axis_size(axis)
    return lax.all_to_all(
        jnp.broadcast_to(value[None], (count, *value.shape)), axis, 0, 0, tiled=True
    )


def inner(first, second):
    return lax.dot_general(first, second, (((0,), (0,)), ((), ())), preferred_element_type=F32)


def dot(first, second):
    return jnp.dot(first, second, preferred_element_type=F32)


def pair_kernel(
    place,
    mine_ref,
    theirs_ref,
    labels_ref,
    gain_ref,
    bias_ref,
    w_in_ref,
    b_in_ref,
    w_out_ref,
    w_bins_ref,
    w_in_t_ref,
    w_out_t_ref,
    w_bins_t_ref,
    weight_out,
    kept_out,
    sent_out,
    blk,
    blk_center,
    far_side,
    far_center,
    label_rows,
    grad_in,
    grad_out_t,
    grad_bins,
    side_sums,
    *,
    count,
    rows,
):
    block = count * rows
    half = block // 2
    width = gain_ref.shape[1]
    beyond = half + GROUP
    twin = place[0] == place[1]
    skew = (place[0] > place[1]).astype(jnp.int32)

    for m in range(count):
        one = mine_ref[m].astype(F32)
        other = theirs_ref[m].astype(F32)
        for side in range(2):
            at = side * GROUP
            blk[side, m * rows : (m + 1) * rows, :] = one[at : at + rows]
            far_side[side, m * rows : (m + 1) * rows, :] = other[at : at + rows]
    label_rows[0:block, :] = labels_ref[...]
    label_rows[block:, :] = labels_ref[0:beyond, :]
    for side in range(2):
        value = blk[side]
        blk_center[side] = value - jnp.mean(value, axis=-1, keepdims=True)
        value = far_side[side, 0:block, :]
        value = value - jnp.mean(value, axis=-1, keepdims=True)
        far_center[side, 0:block, :] = value
        far_center[side, block:, :] = value[0:beyond]
        far_side[side, block:, :] = far_side[side, 0:beyond, :]

    grad_in[...] = jnp.zeros_like(grad_in)
    grad_out_t[...] = jnp.zeros_like(grad_out_t)
    grad_bins[...] = jnp.zeros_like(grad_bins)
    side_sums[...] = jnp.zeros_like(side_sums)

    gain = gain_ref[...]
    bias = bias_ref[...]
    sub = lax.broadcasted_iota(jnp.int32, (GROUP, width), 0)
    lane = lax.broadcasted_iota(jnp.int32, (GROUP, width), 1)
    near = [sub >= ii + skew for ii in range(GROUP)]
    bin_lane = lax.broadcasted_iota(jnp.int32, (GROUP, w_bins_ref.shape[1]), 1).astype(F32)
    span = GROUP * half
    every = span + GROUP

    def step(s, carry):
        first = pl.multiple_of(s * GROUP, GROUP)

        def head(ref, *lead):
            return ref[(*lead, pl.ds(first, GROUP), slice(None))]

        def middle(ref, *lead):
            return ref[(*lead, pl.ds(first + GROUP, half - GROUP), slice(None))]

        def away(ref, *lead):
            return ref[(*lead, pl.ds(first + half, GROUP), slice(None))]

        summed, center = [], []
        for mine, other, into in ((blk, far_side, summed), (blk_center, far_center, center)):
            for side in range(2):
                own = head(mine, side)
                close, apart = head(other, 1 - side), away(other, 1 - side)
                rest = middle(other, 1 - side) if half > GROUP else None
                for ii in range(GROUP):
                    one = own[ii : ii + 1, :]
                    into.append(jnp.where(near[ii], close, apart) + one)
                    if half > GROUP:
                        into.append(rest + one)
                into.append(own + apart)
        summed = jnp.concatenate(summed, axis=0)
        center = jnp.concatenate(center, axis=0)
        inv_scale = lax.rsqrt(jnp.mean(center * center, axis=-1, keepdims=True) + 1e-05)
        normal_form = center * inv_scale
        normed = (normal_form * gain + bias).astype(BF16)
        act = dot(normed, w_in_ref[...]) + b_in_ref[...]
        up = jnp.tanh(act) + 1.0
        hidden = (act * up).astype(BF16)
        slope = up * (act * (2.0 - up) + 1.0)
        updated = (summed + dot(hidden, w_out_ref[...])).astype(BF16)
        logits = dot(updated, w_bins_ref[...])
        sym = logits[0:every] + logits[every:]

        hots, scales = [], []
        label_close, label_apart = head(label_rows), away(label_rows)
        if half > GROUP:
            label_rest = middle(label_rows)
            wide = lax.broadcasted_iota(jnp.int32, label_rest.shape, 1)
            plain = jnp.full((half - GROUP, 1), 2.0, F32)
        for ii in range(GROUP):
            chosen = jnp.where(near[ii], label_close, label_apart)
            hots.append(
                jnp.sum(jnp.where(lane == first + ii, chosen, 0.0), axis=-1, keepdims=True)
            )
            scales.append(jnp.where((sub[:, 0:1] == ii) & twin, 1.0, 2.0))
            if half > GROUP:
                hots.append(
                    jnp.sum(jnp.where(wide == first + ii, label_rest, 0.0), axis=-1, keepdims=True)
                )
                scales.append(plain)
        hots.append(
            jnp.sum(jnp.where(lane == first + sub, label_apart, 0.0), axis=-1, keepdims=True)
        )
        scales.append(jnp.where((sub[:, 0:1] >= 0) & twin, 1.0, 0.0))
        hot = jnp.concatenate(hots, axis=0)
        scale = jnp.concatenate(scales, axis=0)
        lanes = jnp.broadcast_to(bin_lane[0:1], sym.shape)
        expo = jnp.exp(sym - jnp.max(sym, axis=-1, keepdims=True))
        probs = expo / jnp.sum(expo, axis=-1, keepdims=True)
        logit_grad = (scale * (probs - jnp.where(lanes == hot, 1.0, 0.0))).astype(BF16)

        upd_grad = dot(logit_grad, w_bins_t_ref[...])
        upd_half = upd_grad.astype(BF16)
        grad_bins[...] += inner(updated[0:every], logit_grad) + inner(updated[every:], logit_grad)
        grad_out_t[...] += inner(upd_half, hidden[0:every]) + inner(upd_half, hidden[every:])
        hid_grad = dot(upd_half, w_out_t_ref[...])
        pre_grad = jnp.concatenate(
            [(hid_grad * slope[0:every]).astype(BF16), (hid_grad * slope[every:]).astype(BF16)],
            axis=0,
        )
        grad_in[...] += inner(normed, pre_grad)
        norm_grad = dot(pre_grad, w_in_t_ref[...]) * gain
        pair_grad = inv_scale * (
            norm_grad
            - jnp.mean(norm_grad, axis=-1, keepdims=True)
            - normal_form * jnp.mean(norm_grad * normal_form, axis=-1, keepdims=True)
        )
        for side in range(2):
            mine = pair_grad[side * every : (side + 1) * every] + upd_grad
            ones, head_near, head_far, tail = [], None, None, None
            for ii in range(GROUP):
                part = mine[ii * half : (ii + 1) * half]
                ones.append(jnp.sum(part, axis=0, keepdims=True))
                close = jnp.where(near[ii], part[0:GROUP], 0.0)
                apart = part[0:GROUP] - close
                head_near = close if ii == 0 else head_near + close
                head_far = apart if ii == 0 else head_far + apart
                if half > GROUP:
                    tail = part[GROUP:] if ii == 0 else tail + part[GROUP:]
            target = kept_out if side == 0 else sent_out
            target[side, pl.ds(first, GROUP), :] = jnp.concatenate(ones, axis=0) + mine[span:]
            side_sums[1 - side, pl.ds(first, GROUP), :] += head_near
            side_sums[1 - side, pl.ds(first + half, GROUP), :] += head_far + mine[span:]
            if half > GROUP:
                side_sums[1 - side, pl.ds(first + GROUP, half - GROUP), :] += tail
        return carry

    lax.fori_loop(0, block // GROUP, step, 0)

    for side in range(2):
        target = sent_out if side == 0 else kept_out
        target[side, 0:beyond, :] = side_sums[side, 0:beyond, :] + side_sums[side, block:, :]
        target[side, beyond:, :] = side_sums[side, beyond:block, :]

    share_in = grad_in.shape[0] // count
    share_out = grad_out_t.shape[1] // count
    tiles = grad_in.shape[1] // width
    grad_out = grad_out_t[...].T
    bins = grad_bins[...]
    bins = jnp.concatenate([bins, jnp.zeros_like(bins)], axis=1)
    for m in range(count):
        at = 0
        for t in range(tiles):
            weight_out[m, at : at + share_in, :] = grad_in[
                m * share_in : (m + 1) * share_in, t * width : (t + 1) * width
            ]
            at += share_in
        weight_out[m, at : at + share_out, :] = grad_out[m * share_out : (m + 1) * share_out]
        at += share_out
        weight_out[m, at : at + share_in, :] = bins[m * share_in : (m + 1) * share_in]


def run_pairs(place, mine, theirs, rows, labels, gain, bias, w_in, b_in, w_out, w_bins):
    count = mine.shape[0]
    width, hidden = w_in.shape
    bins = w_bins.shape[1]
    block = count * rows
    long = block + block // 2 + GROUP
    share = (width // count) * (hidden // width) + hidden // count + width // count
    vmem = pl.BlockSpec(memory_space=pltpu.VMEM)
    smem = pl.BlockSpec(memory_space=pltpu.SMEM)
    return pl.pallas_call(
        functools.partial(pair_kernel, count=count, rows=rows),
        out_shape=(
            jax.ShapeDtypeStruct((count, share, width), F32),
            jax.ShapeDtypeStruct((2, block, width), F32),
            jax.ShapeDtypeStruct((2, block, width), F32),
        ),
        in_specs=[smem] + [vmem] * 12,
        out_specs=(vmem, vmem, vmem),
        scratch_shapes=[
            pltpu.VMEM((2, block, width), F32),
            pltpu.VMEM((2, block, width), F32),
            pltpu.VMEM((2, long, width), F32),
            pltpu.VMEM((2, long, width), F32),
            pltpu.VMEM((long, width), F32),
            pltpu.VMEM((width, hidden), F32),
            pltpu.VMEM((width, hidden), F32),
            pltpu.VMEM((width, bins), F32),
            pltpu.VMEM((2, long, width), F32),
        ],
        compiler_params=pltpu.CompilerParams(vmem_limit_bytes=56 * 1024 * 1024),
        interpret=INTERPRET,
        name="pairs",
    )(
        place,
        mine,
        theirs,
        labels,
        gain[None],
        bias[None],
        w_in * jnp.asarray(0.5, BF16),
        0.5 * b_in[None],
        w_out,
        w_bins,
        w_in.T,
        w_out.T * jnp.asarray(0.5, BF16),
        w_bins.T,
    )


INTERPRET = False


def on_device(left_act, right_act, norm_gain, norm_bias, w_in, b_in, w_out, w_bins, labels):
    count = lax.axis_size("col")
    size = lax.axis_size("row")
    rows, width = left_act.shape
    hidden = w_in.shape[1]
    swap = [(a * count + b, b * count + a) for a in range(size) for b in range(count)]
    gap = jnp.zeros((GROUP - rows, width), left_act.dtype)
    stacked = jnp.concatenate([left_act, gap, right_act, gap], axis=0)
    mine = from_everyone(stacked, "col")
    theirs = lax.ppermute(mine, ("row", "col"), swap)
    turned = jnp.pad(labels.T.astype(F32), ((0, 0), (0, width - labels.shape[0])))
    place = jnp.stack([lax.axis_index("row"), lax.axis_index("col")]).astype(jnp.int32)
    weight_out, kept, sent = run_pairs(
        place, mine, theirs, rows, turned, norm_gain, norm_bias, w_in, b_in, w_out, w_bins
    )
    kept = kept + lax.ppermute(sent, ("row", "col"), swap)
    shares = lax.all_to_all(weight_out, "col", 0, 0, tiled=True).sum(axis=0)
    share = shares.shape[0]
    piece = -(-share // size)
    shares = jnp.pad(shares, ((0, piece * size - share), (0, 0)))
    pieces = jnp.concatenate(
        [shares.reshape(size, piece, width), kept[1].reshape(size, rows, width)], axis=1
    )
    pieces = lax.all_to_all(pieces, "row", 0, 0, tiled=True).sum(axis=0)
    scale = jnp.where(
        lax.broadcasted_iota(jnp.int32, pieces.shape, 0) < piece, 1.0 / (rows * count * size), 1.0
    )
    pieces = from_everyone(pieces * scale, "row")
    grad_right = pieces[:, piece:].reshape(rows * size, width)
    shares = pieces[:, 0:piece].reshape(size * piece, width)[0:share]
    last = jnp.concatenate(
        [
            jnp.broadcast_to(shares[None], (count, share, width)),
            kept[0].reshape(count, rows, width),
        ],
        axis=1,
    )
    last = lax.all_to_all(last, "col", 0, 0, tiled=True)
    grad_left = last[:, share:].sum(axis=0)
    cut = (width // count) * (hidden // width)
    grad_in = (
        last[:, 0:cut]
        .reshape(count, hidden // width, width // count, width)
        .transpose(0, 2, 1, 3)
        .reshape(width, hidden)
    )
    grad_out = last[:, cut : cut + hidden // count].reshape(hidden, width)
    grad_bins = last[:, cut + hidden // count : share, 0 : w_bins.shape[1]].reshape(width, -1)
    return (grad_left, grad_right, grad_in, grad_out, grad_bins)


def solution(mesh):
    placed = (
        P(("row", "col"), None),
        P(("row", "col"), None),
        P(),
        P(),
        P(),
        P(),
        P(),
        P(),
        P("row", "col"),
    )
    return jax.shard_map(
        on_device,
        mesh=mesh,
        in_specs=placed,
        out_specs=(P(("row", "col"), None), P("col", None), P(), P(), P()),
        check_vma=False,
    )
```

time: 162 us -> 141 us (0.87)
  blocking collectives: 16.2 us -> 0 us
  waiting for transfers between devices: 47.2 us -> 41.7 us
  starting transfers between devices: 44.8 us -> 49 us
  local copies, waits for them, and re-layouts: 9.19 us -> 6.66 us
    all_to_all x2 -> x3, starting transfers between devices: 10.4 us -> 30.5 us  [the longest x1 12.5 us: on_device(): shares = lax.all_to_all(weight_out, 'col', 0, 0, tiled=True).sum(axis=0)]
    all_to_all x4 -> x2, starting transfers between devices: 28.7 us -> 10.7 us  [from_everyone(): lax.all_to_all(jnp.broadcast_to(value[None], (count, *value.shape)), axis...]
    all_to_all x1 -> x0, blocking collectives: 16.2 us -> none  [on_device(): by_col = lax.all_to_all(col_out, 'col', 0, 0, tiled=True).sum(axis=0)]
    all_to_all x4 -> x2, waiting for transfers between devices: 25 us -> 11 us  [from_everyone(): lax.all_to_all(jnp.broadcast_to(value[None], (count, *value.shape)), axis...]
    all_to_all x2 -> x3, waiting for transfers between devices: 12.7 us -> 24 us  [the longest x1 10.6 us: on_device(): last = lax.all_to_all(last, 'col', 0, 0, tiled=True)]
    ppermute x1 -> x2, waiting for transfers between devices: 9.6 us -> 6.73 us  [the longest x1 5.42 us: on_device(): kept = kept + lax.ppermute(sent, ('row', 'col'), swap)]
    ppermute x1 -> x2, starting transfers between devices: 5.6 us -> 7.91 us  [the longest x1 5.21 us: on_device(): theirs = lax.ppermute(mine, ('row', 'col'), swap)]
    unnamed x17 -> x23, local copies, waits for them, and re-layouts: 4.08 us -> 3.14 us
  transfers between devices with their start and end apart: 7 -> 7, of which waited for: 7 -> 7; matrix products, arithmetic and copies ran while one was open for 5% -> 4% of each run, Pallas kernels for 0% -> 0%
where the time goes in v2:
time: 141 us; the launch traced here: 140 us
  starting transfers between devices  49 us (35%)
  waiting for transfers between devices  41.7 us (30%)
  Pallas kernels  36.4 us (26%)
  local copies, waits for them, and re-layouts  6.66 us (5%)
  other arithmetic  5.6 us (4%)
    pallas_call x1, Pallas kernels, run_pairs(): pl.pallas_call(functools.partial(pair_kernel, count=count, rows=rows), ou...  36.4 us
    all_to_all x1, starting transfers between devices, on_device(): shares = lax.all_to_all(weight_out, 'col', 0, 0, tiled=True).sum(axis=0)  12.5 us
    all_to_all x1, starting transfers between devices, on_device(): pieces = lax.all_to_all(pieces, 'row', 0, 0, tiled=True).sum(axis=0)  11.4 us
    all_to_all x2, waiting for transfers between devices, from_everyone(): lax.all_to_all(jnp.broadcast_to(value[None], (count, *value.shape)), axis...  11 us
    all_to_all x2, starting transfers between devices, from_everyone(): lax.all_to_all(jnp.broadcast_to(value[None], (count, *value.shape)), axis...  10.7 us
    all_to_all x1, waiting for transfers between devices, on_device(): last = lax.all_to_all(last, 'col', 0, 0, tiled=True)  10.6 us
    all_to_all x1, waiting for transfers between devices, on_device(): pieces = lax.all_to_all(pieces, 'row', 0, 0, tiled=True).sum(axis=0)  9.85 us
    all_to_all x1, starting transfers between devices, on_device(): last = lax.all_to_all(last, 'col', 0, 0, tiled=True)  6.5 us
  transfers between devices with their start and end apart: 7, of which 7 were waited for; matrix products, arithmetic and copies ran while one was open for 4% of the time, Pallas kernels for 0%

profile of v2, /device:TPU:1, one launch (start us, length us, event | category | flops | bytes accessed | tf_op | source)
XLA Modules:
  0.0 140.2 jit_solution(16040971652079043875)
XLA Ops:
  0.6 0.0 copy-start
  0.7 0.7 pad_maximum_fusion.2
  1.4 0.6 broadcast_in_dim.37
  2.0 7.2 %all-to-all-start = ((bf16[16,16,128]{2,1,0:T(8,128)(2,1)}), bf16[16,16,128]{2,1,0:T(8,128)(2,1)S(1)}, u32[]{:S(2)}, u32[]{:S(2)}) async-start(bf16[16,16,128]{2,1,0:T(8,128)(2,1)} %broadcast_in_dim.37), calls=%async_computation | async-start | bytes 131072 | tf_op jit(solution)/shard_map/all_to_all | solution.py:17
  9.2 0.0 copy-done
  9.2 0.8 copy.23
  9.9 0.0 copy-start.5
  10.0 0.0 copy-start.6
  10.0 0.7 broadcast_multiply_fusion.w_in_ref
  10.6 0.0 copy-start.1
  10.6 0.0 copy-done.5
  10.7 0.7 copy.25.w_bins_ref
  11.4 0.0 copy-done.6
  11.4 0.1 copy.22
  11.5 0.0 copy-done.1
  11.5 0.1 copy.24
  11.7 0.7 multiply_bitcast_fusion.w_out_t_ref
  12.3 0.0 copy-start.7
  12.3 0.6 pad.8.labels_ref
  12.9 0.1 copy-done.7
  13.0 0.6 broadcast_multiply_fusion.2
  13.6 1.4 %all-to-all-done.mine_ref = bf16[16,16,128]{2,1,0:T(8,128)(2,1)S(1)} async-done(((bf16[16,16,128]{2,1,0:T(8,128)(2,1)}), bf16[16,16,128]{2,1,0:T(8,128)(2,1)S(1)}, u32[]{:S(2)}, u32[]{:S(2)}) %all-to-all-start) | async-done | bytes 65568 | tf_op jit(solution)/shard_map/all_to_all | solution.py:17
  15.0 5.2 %collective-permute-start = (bf16[16,16,128]{2,1,0:T(8,128)(2,1)S(1)}, bf16[16,16,128]{2,1,0:T(8,128)(2,1)S(1)}, u32[]{:S(2)}, u32[]{:S(2)}) collective-permute-start(bf16[16,16,128]{2,1,0:T(8,128)(2,1)S(1)} %all-to-all-done.mine_ref), channel_id=1, source_target_pairs={{0,0},{1,16},{2,32},{3,48},{4,64},{5,80},{6,96},{7,112},{8,128},{9... | collective-permute-start | bytes 196616 | tf_op jit(solution)/shard_map/ppermute | solution.py:286
  20.2 0.6 pad_add_fusion.place
  20.9 1.3 collective-permute-done.theirs_ref
  22.2 0.0 copy-done.2
  22.2 0.6 copy-done.4
  22.8 36.4 %pairs.1 = (f32[16,72,128]{2,1,0:T(8,128)}, f32[2,96,128]{2,1,0:T(8,128)}, f32[2,96,128]{2,1,0:T(8,128)}) custom-call(s32[2]{0:T(128)} %pad_add_fusion.place, bf16[16,16,128]{2,1,0:T(8,128)(2,1)} %copy-done.2, bf16[16,16,128]{2,1,0:T(8,128)(2,1)} %copy-done.4, f32[96,128]{1,0:T(8,128)} %pad.8.labels_ref, f32[1,128]{1,0:T(1,128)} %bitcast.24, ...), custom_call_target="tpu_custom_call" | custom-call | tf_op jit(solution)/shard_map/pairs/pallas_call | solution.py:234
  59.1 12.5 %all-to-all-start.1 = ((f32[16,72,128]{2,1,0:T(8,128)}), f32[16,72,128]{2,1,0:T(8,128)S(1)}, u32[]{:S(2)}, u32[]{:S(2)}) async-start(f32[16,72,128]{2,1,0:T(8,128)} %get-tuple-element.8), calls=%async_computation.1 | async-start | bytes 1179648 | tf_op jit(solution)/shard_map/all_to_all | solution.py:293
  71.7 0.0 copy-done.8
  71.7 2.7 %collective-permute-start.1 = (f32[2,96,128]{2,1,0:T(8,128)S(1)}, f32[2,96,128]{2,1,0:T(8,128)S(1)}, u32[]{:S(2)}, u32[]{:S(2)}) collective-permute-start(f32[2,96,128]{2,1,0:T(8,128)S(1)} %copy-done.8), channel_id=1, source_target_pairs={{0,0},{1,16},{2,32},{3,48},{4,64},{5,80},{6,96},{7,112},{8,128},{9... | collective-permute-start | bytes 294920 | tf_op jit(solution)/shard_map/ppermute | solution.py:292
  74.4 5.4 %collective-permute-done.1 = f32[2,96,128]{2,1,0:T(8,128)S(1)} collective-permute-done((f32[2,96,128]{2,1,0:T(8,128)S(1)}, f32[2,96,128]{2,1,0:T(8,128)S(1)}, u32[]{:S(2)}, u32[]{:S(2)}) %collective-permute-start.1) | collective-permute-done | bytes 98336 | tf_op jit(solution)/shard_map/ppermute | solution.py:292
  79.8 0.0 copy-done.3
  79.8 3.6 %all-to-all-done.1 = f32[16,72,128]{2,1,0:T(8,128)S(1)} async-done(((f32[16,72,128]{2,1,0:T(8,128)}), f32[16,72,128]{2,1,0:T(8,128)S(1)}, u32[]{:S(2)}, u32[]{:S(2)}) %all-to-all-start.1) | async-done | bytes 589856 | tf_op jit(solution)/shard_map/all_to_all | solution.py:293
  83.5 0.7 pad_maximum_fusion.1
  84.2 11.4 %all-to-all-start.2 = ((f32[16,11,128]{2,1,0:T(8,128)}), f32[16,11,128]{2,1,0:T(8,128)S(1)}, u32[]{:S(2)}, u32[]{:S(2)}) async-start(f32[16,11,128]{2,1,0:T(8,128)} %pad_maximum_fusion.1), calls=%async_computation.2 | async-start | bytes 262144 | tf_op jit(solution)/shard_map/all_to_all | solution.py:300
  95.6 9.8 %all-to-all-done.2 = f32[16,11,128]{2,1,0:T(8,128)S(1)} async-done(((f32[16,11,128]{2,1,0:T(8,128)}), f32[16,11,128]{2,1,0:T(8,128)S(1)}, u32[]{:S(2)}, u32[]{:S(2)}) %all-to-all-start.2) | async-done | bytes 90144 | tf_op jit(solution)/shard_map/all_to_all | solution.py:300
  105.5 0.1 broadcast_multiply_fusion.1
  105.6 0.7 broadcast_in_dim.42
  106.2 3.5 %all-to-all-start.3 = ((f32[16,11,128]{2,1,0:T(8,128)}), f32[16,11,128]{2,1,0:T(8,128)S(1)}, u32[]{:S(2)}, u32[]{:S(2)}) async-start(f32[16,11,128]{2,1,0:T(8,128)} %broadcast_in_dim.42), calls=%async_computation.3 | async-start | bytes 262144 | tf_op jit(solution)/shard_map/all_to_all | solution.py:17
  109.8 9.6 %all-to-all-done.3 = f32[16,11,128]{2,1,0:T(8,128)S(1)} async-done(((f32[16,11,128]{2,1,0:T(8,128)}), f32[16,11,128]{2,1,0:T(8,128)S(1)}, u32[]{:S(2)}, u32[]{:S(2)}) %all-to-all-start.3) | async-done | bytes 90144 | tf_op jit(solution)/shard_map/all_to_all | solution.py:17
  119.4 0.9 pad_maximum_fusion
  120.3 6.5 %all-to-all-start.4 = ((f32[16,78,128]{2,1,0:T(8,128)}), f32[16,78,128]{2,1,0:T(8,128)S(1)}, u32[]{:S(2)}, u32[]{:S(2)}) async-start(f32[16,78,128]{2,1,0:T(8,128)} %pad_maximum_fusion), calls=%async_computation.4 | async-start | bytes 1310720 | tf_op jit(solution)/shard_map/all_to_all | solution.py:314
  126.8 0.6 reshape.48
  127.4 10.6 %all-to-all-done.4 = f32[16,78,128]{2,1,0:T(8,128)S(1)} async-done(((f32[16,78,128]{2,1,0:T(8,128)}), f32[16,78,128]{2,1,0:T(8,128)S(1)}, u32[]{:S(2)}, u32[]{:S(2)}) %all-to-all-start.4) | async-done | bytes 639008 | tf_op jit(solution)/shard_map/all_to_all | solution.py:314
  138.0 0.7 copy.26
  138.7 0.6 slice_reduce_fusion
  139.3 0.9 fusion
  (21 shorter events, 0.2 us)
Async XLA Ops:
  0.6 8.6 %copy-start = (bf16[128,512]{1,0:T(8,128)(2,1)S(1)}, bf16[128,512]{1,0:T(8,128)(2,1)}, u32[]{:S(2)}) copy-start(bf16[128,512]{1,0:T(8,128)(2,1)} %param.13) | copy-start | bytes 393220
  2.0 13.0 %all-to-all-start = ((bf16[16,16,128]{2,1,0:T(8,128)(2,1)}), bf16[16,16,128]{2,1,0:T(8,128)(2,1)S(1)}, u32[]{:S(2)}, u32[]{:S(2)}) async-start(bf16[16,16,128]{2,1,0:T(8,128)(2,1)} %broadcast_in_dim.37), calls=%async_computation | async-start | bytes 131072 | tf_op jit(solution)/shard_map/all_to_all | solution.py:17
  9.9 0.7 copy-start.5
  10.0 1.4 %copy-start.6 = (s32[96,96]{1,0:T(8,128)S(1)}, s32[96,96]{1,0:T(8,128)}, u32[]{:S(2)}) copy-start(s32[96,96]{1,0:T(8,128)} %param.17) | copy-start | bytes 110596
  10.6 0.9 copy-start.1
  12.3 0.7 copy-start.7
  15.0 7.2 %copy-start.2 = (bf16[16,16,128]{2,1,0:T(8,128)(2,1)}, bf16[16,16,128]{2,1,0:T(8,128)(2,1)S(1)}, u32[]{:S(2)}) copy-start(bf16[16,16,128]{2,1,0:T(8,128)(2,1)S(1)} %all-to-all-done.mine_ref) | copy-start | bytes 196612
  15.0 7.2 %collective-permute-start = (bf16[16,16,128]{2,1,0:T(8,128)(2,1)S(1)}, bf16[16,16,128]{2,1,0:T(8,128)(2,1)S(1)}, u32[]{:S(2)}, u32[]{:S(2)}) collective-permute-start(bf16[16,16,128]{2,1,0:T(8,128)(2,1)S(1)} %all-to-all-done.mine_ref), channel_id=1, source_target_pairs={{0,0},{1,16},{2,32},{3,48},{4,64},{5,80},{6,96},{7,112},{8,128},{9... | collective-permute-start | bytes 196616 | tf_op jit(solution)/shard_map/ppermute | solution.py:286
  22.2 0.6 copy-start.4
  59.1 12.5 %copy-start.8 = (f32[2,96,128]{2,1,0:T(8,128)S(1)}, f32[2,96,128]{2,1,0:T(8,128)}, u32[]{:S(2)}) copy-start(f32[2,96,128]{2,1,0:T(8,128)} %get-tuple-element.10) | copy-start | bytes 294916
  59.1 20.7 %copy-start.3 = (f32[2,96,128]{2,1,0:T(8,128)S(1)}, f32[2,96,128]{2,1,0:T(8,128)}, u32[]{:S(2)}) copy-start(f32[2,96,128]{2,1,0:T(8,128)} %get-tuple-element.9) | copy-start | bytes 294916
  59.1 24.3 %all-to-all-start.1 = ((f32[16,72,128]{2,1,0:T(8,128)}), f32[16,72,128]{2,1,0:T(8,128)S(1)}, u32[]{:S(2)}, u32[]{:S(2)}) async-start(f32[16,72,128]{2,1,0:T(8,128)} %get-tuple-element.8), calls=%async_computation.1 | async-start | bytes 1179648 | tf_op jit(solution)/shard_map/all_to_all | solution.py:293
  71.7 8.1 %collective-permute-start.1 = (f32[2,96,128]{2,1,0:T(8,128)S(1)}, f32[2,96,128]{2,1,0:T(8,128)S(1)}, u32[]{:S(2)}, u32[]{:S(2)}) collective-permute-start(f32[2,96,128]{2,1,0:T(8,128)S(1)} %copy-done.8), channel_id=1, source_target_pairs={{0,0},{1,16},{2,32},{3,48},{4,64},{5,80},{6,96},{7,112},{8,128},{9... | collective-permute-start | bytes 294920 | tf_op jit(solution)/shard_map/ppermute | solution.py:292
  84.2 21.3 %all-to-all-start.2 = ((f32[16,11,128]{2,1,0:T(8,128)}), f32[16,11,128]{2,1,0:T(8,128)S(1)}, u32[]{:S(2)}, u32[]{:S(2)}) async-start(f32[16,11,128]{2,1,0:T(8,128)} %pad_maximum_fusion.1), calls=%async_computation.2 | async-start | bytes 262144 | tf_op jit(solution)/shard_map/all_to_all | solution.py:300
  106.2 13.1 %all-to-all-start.3 = ((f32[16,11,128]{2,1,0:T(8,128)}), f32[16,11,128]{2,1,0:T(8,128)S(1)}, u32[]{:S(2)}, u32[]{:S(2)}) async-start(f32[16,11,128]{2,1,0:T(8,128)} %broadcast_in_dim.42), calls=%async_computation.3 | async-start | bytes 262144 | tf_op jit(solution)/shard_map/all_to_all | solution.py:17
  120.3 17.7 %all-to-all-start.4 = ((f32[16,78,128]{2,1,0:T(8,128)}), f32[16,78,128]{2,1,0:T(8,128)S(1)}, u32[]{:S(2)}, u32[]{:S(2)}) async-start(f32[16,78,128]{2,1,0:T(8,128)} %pad_maximum_fusion), calls=%async_computation.4 | async-start | bytes 1310720 | tf_op jit(solution)/shard_map/all_to_all | solution.py:314

commit v3 on v2

--- a/solution.py
+++ b/solution.py
@@ -7,6 +7,7 @@
 from jax.experimental.pallas import tpu as pltpu
 from jax.sharding import PartitionSpec as P
 
+
 GROUP = 8
 F32 = jnp.float32
 BF16 = jnp.bfloat16
@@ -23,8 +24,30 @@
     return lax.dot_general(first, second, (((0,), (0,)), ((), ())), preferred_element_type=F32)
 
 
+def outer(first, second):
+    return lax.dot_general(first, second, (((1,), (1,)), ((), ())), preferred_element_type=F32)
+
+
 def dot(first, second):
     return jnp.dot(first, second, preferred_element_type=F32)
+
+
+def twin_swap(size, count):
+    return [(a * count + b, b * count + a) for a in range(size) for b in range(count)]
+
+
+def block_routes(size, count):
+    if (size, count) != (16, 16):
+        return twin_swap(size, count)
+    pairs = []
+    for r in range(size):
+        for c in range(count):
+            y, z = (r // 4 - c // 4) % 4, (r % 4 - c % 4) % 4
+            low = (c // 2) % 2
+            low = (low, 1, 1 - low, 0)[z]
+            k = 4 * ((c // 4 + 2 - y) % 4) + 2 * low + (z + 1) % 2
+            pairs.append((c * count + k, r * count + c))
+    return pairs
 
 
 def pair_kernel(
@@ -38,12 +61,10 @@
     b_in_ref,
     w_out_ref,
     w_bins_ref,
-    w_in_t_ref,
-    w_out_t_ref,
-    w_bins_t_ref,
-    weight_out,
-    kept_out,
-    sent_out,
+    col_out,
+    row_out,
+    w_in_half,
+    w_out_half,
     blk,
     blk_center,
     far_side,
@@ -52,6 +73,7 @@
     grad_in,
     grad_out_t,
     grad_bins,
+    blk_sums,
     side_sums,
     *,
     count,
@@ -87,8 +109,11 @@
     grad_bins[...] = jnp.zeros_like(grad_bins)
     side_sums[...] = jnp.zeros_like(side_sums)
 
+    w_in_half[...] = w_in_ref[...] * jnp.asarray(0.5, BF16)
+    w_out_half[...] = w_out_ref[...] * jnp.asarray(0.5, BF16)
     gain = gain_ref[...]
     bias = bias_ref[...]
+    b_in = 0.5 * b_in_ref[...]
     sub = lax.broadcasted_iota(jnp.int32, (GROUP, width), 0)
     lane = lax.broadcasted_iota(jnp.int32, (GROUP, width), 1)
     near = [sub >= ii + skew for ii in range(GROUP)]
@@ -125,7 +150,7 @@
         inv_scale = lax.rsqrt(jnp.mean(center * center, axis=-1, keepdims=True) + 1e-05)
         normal_form = center * inv_scale
         normed = (normal_form * gain + bias).astype(BF16)
-        act = dot(normed, w_in_ref[...]) + b_in_ref[...]
+        act = dot(normed, w_in_half[...]) + b_in
         up = jnp.tanh(act) + 1.0
         hidden = (act * up).astype(BF16)
         slope = up * (act * (2.0 - up) + 1.0)
@@ -161,17 +186,17 @@
         probs = expo / jnp.sum(expo, axis=-1, keepdims=True)
         logit_grad = (scale * (probs - jnp.where(lanes == hot, 1.0, 0.0))).astype(BF16)
 
-        upd_grad = dot(logit_grad, w_bins_t_ref[...])
+        upd_grad = outer(logit_grad, w_bins_ref[...])
         upd_half = upd_grad.astype(BF16)
         grad_bins[...] += inner(updated[0:every], logit_grad) + inner(updated[every:], logit_grad)
         grad_out_t[...] += inner(upd_half, hidden[0:every]) + inner(upd_half, hidden[every:])
-        hid_grad = dot(upd_half, w_out_t_ref[...])
+        hid_grad = outer(upd_half, w_out_half[...])
         pre_grad = jnp.concatenate(
             [(hid_grad * slope[0:every]).astype(BF16), (hid_grad * slope[every:]).astype(BF16)],
             axis=0,
         )
         grad_in[...] += inner(normed, pre_grad)
-        norm_grad = dot(pre_grad, w_in_t_ref[...]) * gain
+        norm_grad = outer(pre_grad, w_in_ref[...]) * gain
         pair_grad = inv_scale * (
             norm_grad
             - jnp.mean(norm_grad, axis=-1, keepdims=True)
@@ -189,8 +214,7 @@
                 head_far = apart if ii == 0 else head_far + apart
                 if half > GROUP:
                     tail = part[GROUP:] if ii == 0 else tail + part[GROUP:]
-            target = kept_out if side == 0 else sent_out
-            target[side, pl.ds(first, GROUP), :] = jnp.concatenate(ones, axis=0) + mine[span:]
+            blk_sums[side, pl.ds(first, GROUP), :] = jnp.concatenate(ones, axis=0) + mine[span:]
             side_sums[1 - side, pl.ds(first, GROUP), :] += head_near
             side_sums[1 - side, pl.ds(first + half, GROUP), :] += head_far + mine[span:]
             if half > GROUP:
@@ -200,9 +224,8 @@
     lax.fori_loop(0, block // GROUP, step, 0)
 
     for side in range(2):
-        target = sent_out if side == 0 else kept_out
-        target[side, 0:beyond, :] = side_sums[side, 0:beyond, :] + side_sums[side, block:, :]
-        target[side, beyond:, :] = side_sums[side, beyond:block, :]
+        row_out[side, 0:beyond, :] = side_sums[side, 0:beyond, :] + side_sums[side, block:, :]
+        row_out[side, beyond:, :] = side_sums[side, beyond:block, :]
 
     share_in = grad_in.shape[0] // count
     share_out = grad_out_t.shape[1] // count
@@ -213,13 +236,17 @@
     for m in range(count):
         at = 0
         for t in range(tiles):
-            weight_out[m, at : at + share_in, :] = grad_in[
+            col_out[m, at : at + share_in, :] = grad_in[
                 m * share_in : (m + 1) * share_in, t * width : (t + 1) * width
             ]
             at += share_in
-        weight_out[m, at : at + share_out, :] = grad_out[m * share_out : (m + 1) * share_out]
+        col_out[m, at : at + share_out, :] = grad_out[m * share_out : (m + 1) * share_out]
         at += share_out
-        weight_out[m, at : at + share_in, :] = bins[m * share_in : (m + 1) * share_in]
+        col_out[m, at : at + share_in, :] = bins[m * share_in : (m + 1) * share_in]
+        at += share_in
+        for side in range(2):
+            col_out[m, at : at + rows, :] = blk_sums[side, m * rows : (m + 1) * rows, :]
+            at += rows
 
 
 def run_pairs(place, mine, theirs, rows, labels, gain, bias, w_in, b_in, w_out, w_bins):
@@ -234,13 +261,14 @@
     return pl.pallas_call(
         functools.partial(pair_kernel, count=count, rows=rows),
         out_shape=(
-            jax.ShapeDtypeStruct((count, share, width), F32),
-            jax.ShapeDtypeStruct((2, block, width), F32),
+            jax.ShapeDtypeStruct((count, share + 2 * rows, width), F32),
             jax.ShapeDtypeStruct((2, block, width), F32),
         ),
-        in_specs=[smem] + [vmem] * 12,
-        out_specs=(vmem, vmem, vmem),
+        in_specs=[smem] + [vmem] * 9,
+        out_specs=(vmem, vmem),
         scratch_shapes=[
+            pltpu.VMEM((width, hidden), BF16),
+            pltpu.VMEM((hidden, width), BF16),
             pltpu.VMEM((2, block, width), F32),
             pltpu.VMEM((2, block, width), F32),
             pltpu.VMEM((2, long, width), F32),
@@ -249,6 +277,7 @@
             pltpu.VMEM((width, hidden), F32),
             pltpu.VMEM((width, hidden), F32),
             pltpu.VMEM((width, bins), F32),
+            pltpu.VMEM((2, block, width), F32),
             pltpu.VMEM((2, long, width), F32),
         ],
         compiler_params=pltpu.CompilerParams(vmem_limit_bytes=56 * 1024 * 1024),
@@ -261,13 +290,10 @@
         labels,
         gain[None],
         bias[None],
-        w_in * jnp.asarray(0.5, BF16),
-        0.5 * b_in[None],
+        w_in,
+        b_in[None],
         w_out,
         w_bins,
-        w_in.T,
-        w_out.T * jnp.asarray(0.5, BF16),
-        w_bins.T,
     )
 
 
@@ -279,40 +305,44 @@
     size = lax.axis_size("row")
     rows, width = left_act.shape
     hidden = w_in.shape[1]
-    swap = [(a * count + b, b * count + a) for a in range(size) for b in range(count)]
+    swap = twin_swap(size, count)
+    both = ("row", "col")
     gap = jnp.zeros((GROUP - rows, width), left_act.dtype)
     stacked = jnp.concatenate([left_act, gap, right_act, gap], axis=0)
     mine = from_everyone(stacked, "col")
-    theirs = lax.ppermute(mine, ("row", "col"), swap)
+    theirs = lax.ppermute(mine, both, block_routes(size, count))
     turned = jnp.pad(labels.T.astype(F32), ((0, 0), (0, width - labels.shape[0])))
     place = jnp.stack([lax.axis_index("row"), lax.axis_index("col")]).astype(jnp.int32)
-    weight_out, kept, sent = run_pairs(
+    col_out, row_out = run_pairs(
         place, mine, theirs, rows, turned, norm_gain, norm_bias, w_in, b_in, w_out, w_bins
     )
-    kept = kept + lax.ppermute(sent, ("row", "col"), swap)
-    shares = lax.all_to_all(weight_out, "col", 0, 0, tiled=True).sum(axis=0)
-    share = shares.shape[0]
+    shares = lax.all_to_all(col_out, "col", 0, 0, tiled=True).sum(axis=0)
+    share = shares.shape[0] - 2 * rows
+    near_left, near_right = lax.optimization_barrier(
+        (shares[share : share + rows], shares[share + rows :])
+    )
+    far_right = lax.ppermute(near_right, both, swap)
+    far_right = jnp.pad(far_right, ((-(-share // size), 0), (0, 0)))
+    far_right = lax.optimization_barrier(far_right)
     piece = -(-share // size)
-    shares = jnp.pad(shares, ((0, piece * size - share), (0, 0)))
+    shares = jnp.pad(shares[0:share], ((0, piece * size - share), (0, 0)))
     pieces = jnp.concatenate(
-        [shares.reshape(size, piece, width), kept[1].reshape(size, rows, width)], axis=1
-    )
-    pieces = lax.all_to_all(pieces, "row", 0, 0, tiled=True).sum(axis=0)
-    scale = jnp.where(
-        lax.broadcasted_iota(jnp.int32, pieces.shape, 0) < piece, 1.0 / (rows * count * size), 1.0
-    )
-    pieces = from_everyone(pieces * scale, "row")
-    grad_right = pieces[:, piece:].reshape(rows * size, width)
-    shares = pieces[:, 0:piece].reshape(size * piece, width)[0:share]
-    last = jnp.concatenate(
         [
-            jnp.broadcast_to(shares[None], (count, share, width)),
-            kept[0].reshape(count, rows, width),
+            shares.reshape(size, piece, width) / (rows * count * size),
+            row_out[1].reshape(size, rows, width),
+            row_out[0].reshape(size, rows, width),
         ],
         axis=1,
     )
-    last = lax.all_to_all(last, "col", 0, 0, tiled=True)
-    grad_left = last[:, share:].sum(axis=0)
+    pieces = lax.all_to_all(pieces, "row", 0, 0, tiled=True)
+    pieces = pieces.sum(axis=0)
+    far_left = lax.ppermute(pieces[piece + rows :], both, swap)
+    far_left = jnp.pad(far_left, ((0, GROUP - rows + 1), (0, 0)))
+    grad_left = near_left + lax.optimization_barrier(far_left)[0:rows]
+    pieces = from_everyone(pieces[0 : piece + rows] + far_right, "row")
+    grad_right = pieces[:, piece:].reshape(rows * size, width)
+    last = pieces[:, 0:piece].reshape(size * piece, width)[0:share]
+    last = from_everyone(last, "col")
     cut = (width // count) * (hidden // width)
     grad_in = (
         last[:, 0:cut]
@@ -337,6 +367,7 @@
         P(),
         P("row", "col"),
     )
+
     return jax.shard_map(
         on_device,
         mesh=mesh,

time: 141 us -> 142 us (level)
  the two profiles are of different devices: /device:TPU:1 before, /device:TPU:36 now
where the time goes in v3:
time: 142 us
  starting transfers between devices  54 us (38%)
  Pallas kernels  34.4 us (24%)
  waiting for transfers between devices  30.4 us (21%)
  blocking collectives  13.3 us (9%)
  local copies, waits for them, and re-layouts  5.9 us (4%)
  other arithmetic  2.84 us (2%)
    pallas_call x1, Pallas kernels, run_pairs(): pl.pallas_call(functools.partial(pair_kernel, count=count, rows=rows), ou...  34.4 us
    all_to_all x2, starting transfers between devices, from_everyone(): lax.all_to_all(jnp.broadcast_to(value[None], (count, *value.shape)), axis...  18 us
    all_to_all x1, blocking collectives, from_everyone(): lax.all_to_all(jnp.broadcast_to(value[None], (count, *value.shape)), axis...  13.3 us
    ppermute x1, starting transfers between devices, on_device(): far_right = lax.ppermute(near_right, both, swap)  12.3 us
    ppermute x1, waiting for transfers between devices, on_device(): far_left = lax.ppermute(pieces[piece + rows:], both, swap)  11.2 us
    all_to_all x1, waiting for transfers between devices, on_device(): shares = lax.all_to_all(col_out, 'col', 0, 0, tiled=True).sum(axis=0)  9.39 us
    all_to_all x1, starting transfers between devices, on_device(): pieces = lax.all_to_all(pieces, 'row', 0, 0, tiled=True)  8.51 us
    all_to_all x1, starting transfers between devices, on_device(): shares = lax.all_to_all(col_out, 'col', 0, 0, tiled=True).sum(axis=0)  8.04 us
  transfers between devices with their start and end apart: 7, of which 5 were waited for; matrix products, arithmetic and copies ran while one was open for 2% of the time, Pallas kernels for 0%

profile of v3, /device:TPU:36, one launch (start us, length us, event | category | flops | bytes accessed | tf_op | source)
XLA Modules:
  0.0 141.6 jit_solution(14759028181472866151)
XLA Ops:
  0.6 0.7 pad_maximum_fusion.1
  1.4 0.6 broadcast_in_dim.15
  2.0 0.0 copy-start.4
  2.0 5.9 %all-to-all-start = ((bf16[16,16,128]{2,1,0:T(8,128)(2,1)}), bf16[16,16,128]{2,1,0:T(8,128)(2,1)S(1)}, u32[]{:S(2)}, u32[]{:S(2)}) async-start(bf16[16,16,128]{2,1,0:T(8,128)(2,1)} %broadcast_in_dim.15), calls=%async_computation | async-start | bytes 131072 | tf_op jit(solution)/shard_map/all_to_all | solution.py:18
  7.8 0.0 copy-start.3
  7.9 0.0 copy-done.4
  7.9 0.7 copy.20.w_bins_ref
  8.6 0.1 copy-done.3
  8.6 0.1 copy.19
  8.7 0.6 pad.16.labels_ref
  9.4 1.6 %all-to-all-done.mine_ref = bf16[16,16,128]{2,1,0:T(8,128)(2,1)S(1)} async-done(((bf16[16,16,128]{2,1,0:T(8,128)(2,1)}), bf16[16,16,128]{2,1,0:T(8,128)(2,1)S(1)}, u32[]{:S(2)}, u32[]{:S(2)}) %all-to-all-start) | async-done | bytes 65568 | tf_op jit(solution)/shard_map/all_to_all | solution.py:18
  10.9 0.0 copy-start
  10.9 5.0 %collective-permute-start = (bf16[16,16,128]{2,1,0:T(8,128)(2,1)S(1)}, bf16[16,16,128]{2,1,0:T(8,128)(2,1)S(1)}, u32[]{:S(2)}, u32[]{:S(2)}) collective-permute-start(bf16[16,16,128]{2,1,0:T(8,128)(2,1)S(1)} %all-to-all-done.mine_ref), channel_id=1, source_target_pairs={{9,0},{24,1},{41,2},{58,3},{65,4},{80,5},{97,6},{114,7},{137,8},{1... | collective-permute-start | bytes 196616 | tf_op jit(solution)/shard_map/ppermute | solution.py:313
  15.9 0.7 pad_add_fusion.place
  16.6 5.6 %collective-permute-done.theirs_ref = bf16[16,16,128]{2,1,0:T(8,128)(2,1)S(1)} collective-permute-done((bf16[16,16,128]{2,1,0:T(8,128)(2,1)S(1)}, bf16[16,16,128]{2,1,0:T(8,128)(2,1)S(1)}, u32[]{:S(2)}, u32[]{:S(2)}) %collective-permute-start) | collective-permute-done | bytes 65568 | tf_op jit(solution)/shard_map/ppermute | solution.py:313
  22.2 0.0 copy-start.2
  22.2 0.0 copy-done
  22.2 0.6 copy-done.2
  22.8 34.4 %pairs.1 = (f32[16,84,128]{2,1,0:T(8,128)}, f32[2,96,128]{2,1,0:T(8,128)}) custom-call(s32[2]{0:T(128)} %pad_add_fusion.place, bf16[16,16,128]{2,1,0:T(8,128)(2,1)} %copy-done, bf16[16,16,128]{2,1,0:T(8,128)(2,1)} %copy-done.2, f32[96,128]{1,0:T(8,128)} %pad.16.labels_ref, f32[1,128]{1,0:T(1,128)} %bitcast.18, f32[1,128]{1,0:T(1,128)} %bitcast.19, ...), custom_call_target="tpu_custom_call" | custom-call | tf_op jit(solution)/shard_map/pairs/pallas_call | solution.py:261
  57.2 0.0 copy-start.1
  57.2 8.0 %all-to-all-start.1 = ((f32[16,84,128]{2,1,0:T(8,128)}), f32[16,84,128]{2,1,0:T(8,128)S(1)}, u32[]{:S(2)}, u32[]{:S(2)}) async-start(f32[16,84,128]{2,1,0:T(8,128)} %get-tuple-element.9), calls=%async_computation.1 | async-start | bytes 1441792 | tf_op jit(solution)/shard_map/all_to_all | solution.py:319
  65.2 0.0 copy-done.1
  65.3 0.0 copy-start.5
  65.3 9.4 %all-to-all-done.1 = f32[16,84,128]{2,1,0:T(8,128)S(1)} async-done(((f32[16,84,128]{2,1,0:T(8,128)}), f32[16,84,128]{2,1,0:T(8,128)S(1)}, u32[]{:S(2)}, u32[]{:S(2)}) %all-to-all-start.1) | async-done | bytes 688160 | tf_op jit(solution)/shard_map/all_to_all | solution.py:319
  74.7 0.0 copy-done.5
  74.7 0.1 fusion
  74.8 0.7 pad_maximum_fusion
  75.5 8.5 %all-to-all-start.2 = ((f32[16,17,128]{2,1,0:T(8,128)}), f32[16,17,128]{2,1,0:T(8,128)S(1)}, u32[]{:S(2)}, u32[]{:S(2)}) async-start(f32[16,17,128]{2,1,0:T(8,128)} %pad_maximum_fusion), calls=%async_computation.2 | async-start | bytes 393216 | tf_op jit(solution)/shard_map/all_to_all | solution.py:337
  84.1 12.3 %collective-permute-start.2 = (f32[6,128]{1,0:T(8,128)S(1)}, f32[6,128]{1,0:T(8,128)S(1)}, u32[]{:S(2)}, u32[]{:S(2)}) collective-permute-start(f32[6,128]{1,0:T(8,128)S(1)} %get-tuple-element.12), channel_id=1, source_target_pairs={{0,0},{1,16},{2,32},{3,48},{4,64},{5,80},{6,96},{7,112},{8,128},{9... | collective-permute-start | bytes 9224 | tf_op jit(solution)/shard_map/ppermute | solution.py:324
  96.4 2.7 %collective-permute-done.2 = f32[6,128]{1,0:T(8,128)S(1)} collective-permute-done((f32[6,128]{1,0:T(8,128)S(1)}, f32[6,128]{1,0:T(8,128)S(1)}, u32[]{:S(2)}, u32[]{:S(2)}) %collective-permute-start.2) | collective-permute-done | bytes 3104 | tf_op jit(solution)/shard_map/ppermute | solution.py:324
  99.1 0.0 all-to-all-done.2
  99.1 13.3 %all_to_all.25 = f32[16,11,128]{2,1,0:T(8,128)S(1)} all-to-all(f32[16,11,128]{2,1,0:T(8,128)S(1)} %broadcast_in_dim.35), channel_id=1, replica_groups=mesh['row'=16,'col'=16] {'row'}, dimensions={0} | all-to-all | bytes 180224 | tf_op jit(solution)/shard_map/all_to_all | solution.py:18
  112.5 0.9 broadcast_in_dim.36
  113.4 12.1 %all-to-all-start.4 = ((f32[16,72,128]{2,1,0:T(8,128)}), f32[16,72,128]{2,1,0:T(8,128)S(1)}, u32[]{:S(2)}, u32[]{:S(2)}) async-start(f32[16,72,128]{2,1,0:T(8,128)} %broadcast_in_dim.36), calls=%async_computation.4 | async-start | bytes 1179648 | tf_op jit(solution)/shard_map/all_to_all | solution.py:18
  125.5 2.1 %collective-permute-start.1 = (f32[6,128]{1,0:T(8,128)S(1)}, f32[6,128]{1,0:T(8,128)S(1)}, u32[]{:S(2)}, u32[]{:S(2)}) collective-permute-start(f32[6,128]{1,0:T(8,128)S(1)} %slice.60), channel_id=1, source_target_pairs={{0,0},{1,16},{2,32},{3,48},{4,64},{5,80},{6,96},{7,112},{8,128},{9... | collective-permute-start | bytes 9224 | tf_op jit(solution)/shard_map/ppermute | solution.py:339
  127.6 11.2 %collective-permute-done.1 = f32[6,128]{1,0:T(8,128)S(1)} collective-permute-done((f32[6,128]{1,0:T(8,128)S(1)}, f32[6,128]{1,0:T(8,128)S(1)}, u32[]{:S(2)}, u32[]{:S(2)}) %collective-permute-start.1) | collective-permute-done | bytes 3104 | tf_op jit(solution)/shard_map/ppermute | solution.py:339
  138.8 0.6 slice_add_fusion.1
  139.5 0.6 reshape.34
  140.1 0.0 all-to-all-done.4
  140.1 0.7 copy.21
  140.8 0.8 fusion.1
  (19 shorter events, 0.2 us)
Async XLA Ops:
  2.0 5.9 %copy-start.4 = (bf16[128,64]{0,1:T(8,128)(2,1)S(1)}, bf16[128,64]{0,1:T(8,128)(2,1)}, u32[]{:S(2)}) copy-start(bf16[128,64]{0,1:T(8,128)(2,1)} %param.16) | copy-start | bytes 49156
  2.0 8.9 %all-to-all-start = ((bf16[16,16,128]{2,1,0:T(8,128)(2,1)}), bf16[16,16,128]{2,1,0:T(8,128)(2,1)S(1)}, u32[]{:S(2)}, u32[]{:S(2)}) async-start(bf16[16,16,128]{2,1,0:T(8,128)(2,1)} %broadcast_in_dim.15), calls=%async_computation | async-start | bytes 131072 | tf_op jit(solution)/shard_map/all_to_all | solution.py:18
  7.8 0.8 copy-start.3
  10.9 11.2 %copy-start = (bf16[16,16,128]{2,1,0:T(8,128)(2,1)}, bf16[16,16,128]{2,1,0:T(8,128)(2,1)S(1)}, u32[]{:S(2)}) copy-start(bf16[16,16,128]{2,1,0:T(8,128)(2,1)S(1)} %all-to-all-done.mine_ref) | copy-start | bytes 196612
  10.9 11.2 %collective-permute-start = (bf16[16,16,128]{2,1,0:T(8,128)(2,1)S(1)}, bf16[16,16,128]{2,1,0:T(8,128)(2,1)S(1)}, u32[]{:S(2)}, u32[]{:S(2)}) collective-permute-start(bf16[16,16,128]{2,1,0:T(8,128)(2,1)S(1)} %all-to-all-done.mine_ref), channel_id=1, source_target_pairs={{9,0},{24,1},{41,2},{58,3},{65,4},{80,5},{97,6},{114,7},{137,8},{1... | collective-permute-start | bytes 196616 | tf_op jit(solution)/shard_map/ppermute | solution.py:313
  22.2 0.6 copy-start.2
  57.2 8.0 %copy-start.1 = (f32[2,96,128]{2,1,0:T(8,128)S(1)}, f32[2,96,128]{2,1,0:T(8,128)}, u32[]{:S(2)}) copy-start(f32[2,96,128]{2,1,0:T(8,128)} %get-tuple-element.11) | copy-start | bytes 294916
  57.2 17.5 %all-to-all-start.1 = ((f32[16,84,128]{2,1,0:T(8,128)}), f32[16,84,128]{2,1,0:T(8,128)S(1)}, u32[]{:S(2)}, u32[]{:S(2)}) async-start(f32[16,84,128]{2,1,0:T(8,128)} %get-tuple-element.9), calls=%async_computation.1 | async-start | bytes 1441792 | tf_op jit(solution)/shard_map/all_to_all | solution.py:319
  65.3 9.4 %copy-start.5 = (pred[80]{0:T(512)(128)(4,1)S(1)}, pred[80]{0:T(512)(128)(4,1)}, u32[]{:S(2)}) copy-start(pred[80]{0:T(512)(128)(4,1)} %constant.16.clone.1) | copy-start | bytes 244
  75.5 23.5 %all-to-all-start.2 = ((f32[16,17,128]{2,1,0:T(8,128)}), f32[16,17,128]{2,1,0:T(8,128)S(1)}, u32[]{:S(2)}, u32[]{:S(2)}) async-start(f32[16,17,128]{2,1,0:T(8,128)} %pad_maximum_fusion), calls=%async_computation.2 | async-start | bytes 393216 | tf_op jit(solution)/shard_map/all_to_all | solution.py:337
  84.1 15.0 %collective-permute-start.2 = (f32[6,128]{1,0:T(8,128)S(1)}, f32[6,128]{1,0:T(8,128)S(1)}, u32[]{:S(2)}, u32[]{:S(2)}) collective-permute-start(f32[6,128]{1,0:T(8,128)S(1)} %get-tuple-element.12), channel_id=1, source_target_pairs={{0,0},{1,16},{2,32},{3,48},{4,64},{5,80},{6,96},{7,112},{8,128},{9... | collective-permute-start | bytes 9224 | tf_op jit(solution)/shard_map/ppermute | solution.py:324
  113.4 26.7 %all-to-all-start.4 = ((f32[16,72,128]{2,1,0:T(8,128)}), f32[16,72,128]{2,1,0:T(8,128)S(1)}, u32[]{:S(2)}, u32[]{:S(2)}) async-start(f32[16,72,128]{2,1,0:T(8,128)} %broadcast_in_dim.36), calls=%async_computation.4 | async-start | bytes 1179648 | tf_op jit(solution)/shard_map/all_to_all | solution.py:18
  125.5 13.3 %collective-permute-start.1 = (f32[6,128]{1,0:T(8,128)S(1)}, f32[6,128]{1,0:T(8,128)S(1)}, u32[]{:S(2)}, u32[]{:S(2)}) collective-permute-start(f32[6,128]{1,0:T(8,128)S(1)} %slice.60), channel_id=1, source_target_pairs={{0,0},{1,16},{2,32},{3,48},{4,64},{5,80},{6,96},{7,112},{8,128},{9... | collective-permute-start | bytes 9224 | tf_op jit(solution)/shard_map/ppermute | solution.py:339
